TPU v7x, 32 devices: a whole 2x2x4 slice. The times are simulated.
32 devices in a mesh: rep: 1, dp: 32 (over x, y, z, core).
Axes of the slice: x: 2, y: 2, z: 4, core: 2. Of those that a mesh axis runs over, the one named last changes fastest.
Arguments:
- g_w_gate: bfloat16 [32, 2, 1024, 5120], P(('rep', 'dp'))
- g_w_up: bfloat16 [32, 2, 1024, 5120], P(('rep', 'dp'))
- g_w_down: bfloat16 [32, 2, 5120, 1024], P(('rep', 'dp'))
- w_gate: bfloat16 [2, 1024, 5120], replicated
- w_up: bfloat16 [2, 1024, 5120], replicated
- w_down: bfloat16 [2, 5120, 1024], replicated
- m_w_gate: float32 [2, 1024, 5120], P(None, 'dp')
- m_w_up: float32 [2, 1024, 5120], P(None, 'dp')
- m_w_down: float32 [2, 5120, 1024], P(None, 'dp')
- v_w_gate: float32 [2, 1024, 5120], P(None, 'dp')
- v_w_up: float32 [2, 1024, 5120], P(None, 'dp')
- v_w_down: float32 [2, 5120, 1024], P(None, 'dp')
Outputs:
- output 1: bfloat16 [2, 1024, 5120], P('rep')
- output 2: bfloat16 [2, 1024, 5120], P('rep')
- output 3: bfloat16 [2, 5120, 1024], P('rep')
- output 4: float32 [2, 1024, 5120], P('rep', 'dp')
- output 5: float32 [2, 1024, 5120], P('rep', 'dp')
- output 6: float32 [2, 5120, 1024], P('rep', 'dp')
- output 7: float32 [2, 1024, 5120], P('rep', 'dp')
- output 8: float32 [2, 1024, 5120], P('rep', 'dp')
- output 9: float32 [2, 5120, 1024], P('rep', 'dp')
All inputs are finite; a program needn't handle non-finite values.
Results may differ from a plain program's by a relative error of at most 0.022.
Values are sent between devices in bfloat16 or wider.
A program may use at most 2 GiB of HBM per device.

v0:
```python
import jax
import jax.numpy as jnp
from jax import lax
from jax.sharding import PartitionSpec as P


def adamw(w, m, v, g):
    m = 0.9 * m + 0.1 * g
    v = 0.95 * v + 0.05 * g * g
    step = m * lax.rsqrt(v + 1e-8) + 0.1 * w
    return (w - 0.02 * step).astype(jnp.bfloat16), m, v


def clipped(gradients, sum_of_squares, count):
    factor = jnp.minimum(1.0, 0.5 * lax.rsqrt(sum_of_squares / count + 1e-30))
    return [g * factor for g in gradients]


def solution(mesh):
    def step(*arrays):
        terms, weights, m, v = (arrays[i : i + 3] for i in (0, 3, 6, 9))
        gradients = [lax.psum_scatter(t[0], "dp", scatter_dimension=1, tiled=True).astype(jnp.float32) for t in terms]
        squares = lax.psum(sum(jnp.sum(g * g) for g in gradients), "dp")
        gradients = clipped(gradients, squares, lax.psum(1, "dp") * sum(g.size for g in gradients))
        me = lax.axis_index("dp")
        own = [lax.dynamic_slice_in_dim(w, me * one.shape[1], one.shape[1], 1).astype(jnp.float32) for w, one in zip(weights, m, strict=True)]
        new = [adamw(w, m, v, g) for w, m, v, g in zip(own, m, v, gradients, strict=True)]
        whole = [lax.all_gather(one[0], "dp", axis=1, tiled=True) for one in new]
        return (*whole, *(one[1] for one in new), *(one[2] for one in new))

    all_of, cut = P(None, None, None), P(None, "dp", None)
    return jax.shard_map(
        step,
        mesh=mesh,
        in_specs=(P(("rep", "dp"), None, None, None),) * 3 + (all_of,) * 3 + (cut,) * 6,
        out_specs=(P("rep", None, None),) * 3 + (P("rep", "dp", None),) * 6,
        check_vma=False,
    )
```

profile of v0, /device:TPU:0, one launch (start us, length us, event | category | flops | bytes accessed | tf_op | source)
XLA Modules:
  0.0 1199.9 jit_solution(1562522229730203243)
XLA Ops:
  7.2 0.0 reduce-scatter.4.cloned.1.call-start
  7.2 0.7 reduce-scatter.4.cloned.1.call-update
  7.9 0.0 reduce-scatter.6.cloned.1.call-start
  8.0 0.7 reduce-scatter.6.cloned.1.call-update
  8.7 0.0 reduce-scatter.8.cloned.1.call-start
  8.7 0.0 copy-start.4
  8.7 0.7 reduce-scatter.8.cloned.1.call-update
  9.4 0.0 copy-start.3
  9.4 0.0 all-gather.8.cloned.1.call-start
  9.5 233.6 %reduce-scatter.4.cloned.1.call-done = bf16[2,32,5120]{2,1,0:T(8,128)(2,1)} async-done(((bf16[2,1024,5120]{2,1,0:T(8,128)(2,1)}), bf16[2,32,5120]{2,1,0:T(8,128)(2,1)}) %reduce-scatter.4.cloned.1.call-update) | async-done | bytes 655376 | tf_op jit(solution)/shard_map/reduce_scatter | solution.py:22
  243.1 2.0 fusion.9
  245.1 227.4 %reduce-scatter.6.cloned.1.call-done = bf16[2,32,5120]{2,1,0:T(8,128)(2,1)} async-done(((bf16[2,1024,5120]{2,1,0:T(8,128)(2,1)}), bf16[2,32,5120]{2,1,0:T(8,128)(2,1)}) %reduce-scatter.6.cloned.1.call-update) | async-done | bytes 655376 | tf_op jit(solution)/shard_map/reduce_scatter | solution.py:22
  472.5 2.0 fusion.10
  475.8 226.1 %reduce-scatter.8.cloned.1.call-done = bf16[2,160,1024]{2,1,0:T(8,128)(2,1)} async-done(((bf16[2,5120,1024]{2,1,0:T(8,128)(2,1)}), bf16[2,160,1024]{2,1,0:T(8,128)(2,1)}) %reduce-scatter.8.cloned.1.call-update) | async-done | bytes 655376 | tf_op jit(solution)/shard_map/reduce_scatter | solution.py:22
  701.9 2.0 fusion.11
  704.5 36.8 %psum.7 = f32[]{:T(128)} all-reduce(f32[]{:T(128)S(6)} %add.65), channel_id=1, replica_groups=mesh['rep'=1,'dp'=32] {'dp'}, use_global_device_ids=true, to_apply=%region_6.0 | all-reduce | flops 1 | bytes 8 | tf_op jit(solution)/shard_map/psum | solution.py:23
  742.1 0.0 copy-done.4
  742.1 0.0 copy-done.3
  742.1 0.0 copy-start.2
  742.1 3.5 fusion.17
  745.6 0.0 all-gather.8.cloned.1.call-update
  745.6 0.0 all-gather.4.cloned.1.call-start
  745.7 0.0 copy-done.2
  745.7 0.0 copy-start.1
  745.7 0.0 copy-start.5
  745.7 4.1 fusion.8
  749.8 0.0 all-gather.4.cloned.1.call-update
  749.8 0.0 all-gather.6.cloned.1.call-start
  749.9 0.0 copy-done.1
  749.9 0.0 copy-done.5
  749.9 3.6 fusion.14
  753.5 0.0 all-gather.6.cloned.1.call-update
  753.5 126.4 %all-gather.8.cloned.1.call-done = bf16[2,5120,1024]{2,1,0:T(8,128)(2,1)} async-done(((bf16[2,160,1024]{2,1,0:T(8,128)(2,1)}), bf16[2,5120,1024]{2,1,0:T(8,128)(2,1)}) %all-gather.8.cloned.1.call-update) | async-done | bytes 20971536 | tf_op jit(solution)/shard_map/all_gather | solution.py:28
  879.9 135.4 %all-gather.4.cloned.1.call-done = bf16[2,1024,5120]{2,1,0:T(8,128)(2,1)} async-done(((bf16[2,32,5120]{2,1,0:T(8,128)(2,1)}), bf16[2,1024,5120]{2,1,0:T(8,128)(2,1)}) %all-gather.4.cloned.1.call-update) | async-done | bytes 20971536 | tf_op jit(solution)/shard_map/all_gather | solution.py:28
  1015.3 135.4 %all-gather.6.cloned.1.call-done = bf16[2,1024,5120]{2,1,0:T(8,128)(2,1)} async-done(((bf16[2,32,5120]{2,1,0:T(8,128)(2,1)}), bf16[2,1024,5120]{2,1,0:T(8,128)(2,1)}) %all-gather.6.cloned.1.call-update) | async-done | bytes 20971536 | tf_op jit(solution)/shard_map/all_gather | solution.py:28
  1150.8 0.0 copy-start
  1150.8 0.0 slice-start
  1150.8 0.0 slice-start.1
  1150.8 0.0 slice-start.2
  1150.8 20.9 %copy.24 = bf16[2,1024,5120]{2,1,0:T(8,128)(2,1)} copy(bf16[2,1024,5120]{2,1,0:T(8,128)(2,1)} %all-gather.4.cloned.1.call-done) | data formatting | bytes 41943040
  1171.7 0.0 copy-done
  1171.7 0.0 slice-start.3
  1171.7 0.0 slice-start.4
  1171.7 10.6 copy.25
  1182.4 0.0 slice-done
  1182.4 0.0 slice-done.1
  1182.4 0.0 slice-done.2
  1182.4 1.9 slice-done.3
  1184.3 1.2 slice-done.4
  1185.5 7.5 copy.26
  (1 shorter events, 0.0 us)
Async XLA Ops:
  7.2 235.9 %reduce-scatter.4.cloned.1.call-start = ((), (), s32[]{:S(2)}) async-start(), calls=%async_computation.3 | async-start | bytes 21626880 | tf_op jit(solution)/shard_map/reduce_scatter | solution.py:22
  7.9 464.6 %reduce-scatter.6.cloned.1.call-start = ((), (), s32[]{:S(2)}) async-start(), calls=%async_computation.4 | async-start | bytes 21626880 | tf_op jit(solution)/shard_map/reduce_scatter | solution.py:22
  8.7 693.2 %reduce-scatter.8.cloned.1.call-start = ((), (), s32[]{:S(2)}) async-start(), calls=%async_computation.5 | async-start | bytes 21626880 | tf_op jit(solution)/shard_map/reduce_scatter | solution.py:22
  8.7 733.4 %copy-start.4 = (f32[2,160,1024]{2,1,0:T(8,128)S(1)}, f32[2,160,1024]{2,1,0:T(8,128)}, u32[]{:S(2)}) copy-start(f32[2,160,1024]{2,1,0:T(8,128)} %param.20) | copy-start | bytes 3932164
  9.4 732.7 %copy-start.3 = (f32[2,160,1024]{2,1,0:T(8,128)S(1)}, f32[2,160,1024]{2,1,0:T(8,128)}, u32[]{:S(2)}) copy-start(f32[2,160,1024]{2,1,0:T(8,128)} %param.23) | copy-start | bytes 3932164
  9.4 870.5 %all-gather.8.cloned.1.call-start = ((), (), s32[]{:S(2)}) async-start(), calls=%async_computation.8 | async-start | bytes 21626880 | tf_op jit(solution)/shard_map/all_gather | solution.py:28
  742.1 3.6 copy-start.2
  745.6 269.7 %all-gather.4.cloned.1.call-start = ((), (), s32[]{:S(2)}) async-start(), calls=%async_computation.6 | async-start | bytes 21626880 | tf_op jit(solution)/shard_map/all_gather | solution.py:28
  745.7 4.2 copy-start.1
  745.7 4.2 copy-start.5
  749.8 401.0 %all-gather.6.cloned.1.call-start = ((), (), s32[]{:S(2)}) async-start(), calls=%async_computation.7 | async-start | bytes 21626880 | tf_op jit(solution)/shard_map/all_gather | solution.py:28
  1150.8 21.0 %copy-start = (bf16[2,1024,5120]{2,1,0:T(8,128)(2,1)S(1)}, bf16[2,1024,5120]{2,1,0:T(8,128)(2,1)}, u32[]{:S(2)}) copy-start(bf16[2,1024,5120]{2,1,0:T(8,128)(2,1)} %all-gather.6.cloned.1.call-done) | copy-start | bytes 62914564
  1150.8 31.6 %slice-start = ((s8[20971520]{0:T(1024)(128)(4,1)}), s8[4194304]{0:T(1024)(128)(4,1)S(1)}, s32[]{:S(2)}) async-start(s8[20971520]{0:T(1024)(128)(4,1)} %bitcast.6), calls=%async_computation.9 | async-start | bytes 8388608
  1150.8 31.6 %slice-start.1 = ((s8[20971520]{0:T(1024)(128)(4,1)}), s8[4194304]{0:T(1024)(128)(4,1)S(1)}, s32[]{:S(2)}) async-start(s8[20971520]{0:T(1024)(128)(4,1)} %bitcast.6), calls=%async_computation.10 | async-start | bytes 8388608
  1150.8 31.6 %slice-start.2 = ((s8[20971520]{0:T(1024)(128)(4,1)}), s8[4194304]{0:T(1024)(128)(4,1)S(1)}, s32[]{:S(2)}) async-start(s8[20971520]{0:T(1024)(128)(4,1)} %bitcast.6), calls=%async_computation.11 | async-start | bytes 8388608
  1171.7 12.6 %slice-start.3 = ((s8[20971520]{0:T(1024)(128)(4,1)}), s8[4194304]{0:T(1024)(128)(4,1)S(1)}, s32[]{:S(2)}) async-start(s8[20971520]{0:T(1024)(128)(4,1)} %bitcast.6), calls=%async_computation.12 | async-start | bytes 8388608
  1171.7 13.7 %slice-start.4 = ((s8[20971520]{0:T(1024)(128)(4,1)}), s8[4194304]{0:T(1024)(128)(4,1)S(1)}, s32[]{:S(2)}) async-start(s8[20971520]{0:T(1024)(128)(4,1)} %bitcast.6), calls=%async_computation.13 | async-start | bytes 8388608
Sparse Core Ops, SparseCore 0:
  10.3 232.7 reduce-scatter.3
  245.4 227.0 reduce-scatter.5
  474.8 227.0 reduce-scatter.7
  745.7 134.1 all-gather.7
  883.3 131.9 all-gather.3
  1018.7 131.9 all-gather.5
where the time goes:
time: 1200 us
  waiting for transfers between devices  1090 us (91%)
  local copies, waits for them, and re-layouts  42.3 us (4%)
  blocking collectives  36.8 us (3%)
  other arithmetic  17.2 us (1%)
  between operations  16.9 us (1%)
    reduce_scatter x3, waiting for transfers between devices, step(): lax.psum_scatter(t[0], 'dp', scatter_dimension=1, tiled=True)  687 us
    all_gather x3, waiting for transfers between devices, step(): whole = [lax.all_gather(one[0], 'dp', axis=1, tiled=True) for one in new]  397 us
    unnamed x25, local copies, waits for them, and re-layouts  42.3 us
    psum x1, blocking collectives, step(): squares = lax.psum(sum((jnp.sum(g * g) for g in gradients)), 'dp')  36.8 us
  transfers between devices with their start and end apart: 6, of which 6 were waited for; matrix products, arithmetic and copies ran while one was open for 1% of the time, Pallas kernels for 0%

commit v1 on v0

v1 whole, which is shorter than its diff:
```python
import jax
import jax.numpy as jnp
from jax import lax
from jax.experimental import pallas as pl
from jax.experimental.pallas import tpu as pltpu
from jax.sharding import PartitionSpec as P

MESH = pl.DeviceIdType.MESH
F32, BF16 = jnp.float32, jnp.bfloat16
ANY = pl.BlockSpec(memory_space=pl.ANY)


class Place:
    def __init__(self):
        self.rep, d = lax.axis_index("rep"), lax.axis_index("dp")
        self.x, self.y, self.z, self.c = d // 16, lax.rem(d // 8, 2), lax.rem(d // 2, 4), lax.rem(d, 2)
        low = self.z < 2
        self.low = low
        self.mz = jnp.where(low, self.z, 3 - self.z)
        self.end, self.inner = self.mz == 0, self.mz == 1
        self.far = self.dev(self.x, self.y, jnp.where(low, self.z + 1, self.z - 1), self.c)
        self.near = self.dev(self.x, self.y, jnp.where(low, 0, 3), self.c)
        self.nx = self.dev(1 - self.x, self.y, self.z, self.c)
        self.ny = self.dev(self.x, 1 - self.y, self.z, self.c)
        self.nc = self.dev(self.x, self.y, self.z, 1 - self.c)
        self.qo = self.x * 2 + self.y
        self.qx = (1 - self.x) * 2 + self.y
        self.qy = self.x * 2 + 1 - self.y
        self.qd = (1 - self.x) * 2 + 1 - self.y

    def dev(self, x, y, z, c):
        return (self.rep, ((x * 2 + y) * 4 + z) * 2 + c)

    def zi(self, m):
        return jnp.where(self.low, m, 3 - m)

    def line(self, k):
        return lax.rem(self.z + k, 4)

    def meet(self, peers):
        barrier = pltpu.get_barrier_semaphore()
        for p in peers:
            pl.semaphore_signal(barrier, inc=1, device_id=p, device_id_type=MESH)
        pl.semaphore_wait(barrier, len(peers))


def send(src, dst, s, r, to):
    pltpu.make_async_remote_copy(src_ref=src, dst_ref=dst, send_sem=s, recv_sem=r, device_id=to, device_id_type=MESH).start()


def arrived(ref, sem):
    pltpu.make_async_copy(ref, ref, sem).wait()


def add_into(dst, *srcs):
    rows, cols = dst.shape
    step = 16 if cols > 2048 else 32

    def strip(i, carry):
        at = pl.ds(pl.multiple_of(i * step, step), step)
        total = srcs[0][at, :].astype(F32)
        for s in srcs[1:]:
            total = total + s[at, :].astype(F32)
        dst[at, :] = total.astype(BF16)
        return carry

    lax.fori_loop(0, rows // step, strip, 0)


def each(n, body):
    lax.fori_loop(0, n, lambda i, carry: (body(i), carry)[1], 0)


TASKS = ["D0", "D1", "X0", "Y0", "D2", "X1", "Y1", "D3", "X2", "Y2", "O0", "D4", "X3", "Y3", "O1", "D5", "X4", "Y4", "O2", "X5", "Y5", "O3", "O4", "O5"]


def rs_kernel(*refs):
    terms, outs, theirs, total = refs[0:3], refs[3:6], refs[6:9], refs[9]
    wide, tall = refs[10:19], refs[19:28]
    sq, lz, lg, cs, cr, ls, xs, xr, ys, yr, zs, zr, osem, es, er = refs[28:]
    at = Place()
    group = (at.x * 2 + at.y) * 2 + at.c
    line_peers = [at.dev(at.x, at.y, at.line(k), at.c) for k in (1, 2, 3)]
    others = [lax.rem(group + k, 8) for k in range(1, 8)]
    group_peers = [at.dev(j // 4, lax.rem(j // 2, 2), at.z, lax.rem(j, 2)) for j in others]
    at.meet(line_peers + group_peers)
    columns = {"D": at.qd, "X": at.qx, "Y": at.qy, "O": at.qo}

    def parts(name):
        t = int(name[1])
        bufs = (wide, t) if t < 4 else (tall, t - 4)
        return t, terms[t // 2], theirs[t // 2], t % 2, columns[name[0]], bufs

    for k, name in enumerate(TASKS):
        t, g, p, layer, q, _ = parts(name)
        send(g.at[layer, q, :, 1 - at.c], p.at[layer, q], cs.at[k], cr.at[k], at.nc)

    slots, used = {}, {True: 0, False: 0}
    for name in TASKS:
        kind = int(name[1]) < 4
        slots[name] = used[kind] % 2
        used[kind] += 1

    def stage_of(name):
        t = int(name[1])
        return (wide if t < 4 else tall)[8].at[slots[name]], ls.at[0 if t < 4 else 1, slots[name]]

    def load(k):
        name = TASKS[k]
        t, g, p, layer, q, _ = parts(name)
        stage, sem = stage_of(name)
        pltpu.make_async_copy(g.at[layer, q, :, at.c], stage.at[0], sem.at[0]).start()
        arrived(p.at[layer, q], cr.at[k])
        pltpu.make_async_copy(p.at[layer, q], stage.at[1], sem.at[1]).start()

    sq[...] = jnp.zeros_like(sq)
    load(0)
    for k, name in enumerate(TASKS):
        if k + 1 < len(TASKS):
            load(k + 1)
        t, g, p, layer, q, (bufs, b) = parts(name)
        xf, yf, xin, yin, sd, rx, ry, zin = (r.at[b] for r in bufs[:8])
        stage, sem = stage_of(name)
        arrived(stage.at[0], sem.at[0])
        arrived(stage.at[1], sem.at[1])
        mine, yours = stage.at[0], stage.at[1]
        lower, upper = pl.ds(0, 2), pl.ds(2, 2)
        if name[0] == "D":
            each(4, lambda i: add_into(sd.at[i], mine.at[i], yours.at[i]))
            send(sd.at[lower], xf, xs.at[t, 0], xr.at[t, 0], at.nx)
            send(sd.at[upper], yf, ys.at[t, 0], yr.at[t, 0], at.ny)
        elif name[0] == "X":
            each(2, lambda i: add_into(rx.at[i], mine.at[i], yours.at[i]))
            send(rx, xin.at[lower], xs.at[t, 1], xr.at[t, 1], at.nx)
            arrived(yf, yr.at[t, 0])
            each(2, lambda i: add_into(yf.at[i], mine.at[i + 2], yours.at[i + 2], yf.at[i]))
            send(yf, xin.at[upper], xs.at[t, 2], xr.at[t, 2], at.nx)
        elif name[0] == "Y":
            each(2, lambda i: add_into(ry.at[i], mine.at[i + 2], yours.at[i + 2]))
            send(ry, yin.at[upper], ys.at[t, 1], yr.at[t, 1], at.ny)
            arrived(xf, xr.at[t, 0])
            each(2, lambda i: add_into(xf.at[i], mine.at[i], yours.at[i], xf.at[i]))
            send(xf, yin.at[lower], ys.at[t, 2], yr.at[t, 2], at.ny)
        else:
            arrived(xin.at[lower], xr.at[t, 1])
            arrived(yin.at[upper], yr.at[t, 1])
            arrived(yin.at[lower], yr.at[t, 2])
            arrived(xin.at[upper], xr.at[t, 2])

            def four(i):
                return mine.at[i], yours.at[i], xin.at[i], yin.at[i]

            @pl.when(at.end)
            def _():
                for m in (3, 2, 1):
                    i = at.zi(m)
                    add_into(xin.at[i], *four(i))
                    send(xin.at[i], zin.at[m - 1], zs.at[t, m - 1], zr.at[t, m - 1], at.far)

            @pl.when(at.inner)
            def _():
                for m in (3, 2):
                    i = at.zi(m)
                    arrived(zin.at[m - 1], zr.at[t, m - 1])
                    add_into(zin.at[m - 1], *four(i), zin.at[m - 1])
                    send(zin.at[m - 1], zin.at[6 - m], zs.at[t, m - 1], zr.at[t, 6 - m], at.far)
                i = at.zi(0)
                arrived(zin.at[3], zr.at[t, 3])
                add_into(zin.at[3], *four(i), zin.at[3])
                send(zin.at[3], zin.at[3], zs.at[t, 0], zr.at[t, 3], at.near)

            own = at.z

            @pl.when(at.end)
            def _():
                arrived(zin.at[3], zr.at[t, 3])
                add_into(yin.at[own], *four(own), zin.at[3])

            @pl.when(at.inner)
            def _():
                arrived(zin.at[0], zr.at[t, 0])
                arrived(zin.at[4], zr.at[t, 4])
                add_into(yin.at[own], *four(own), zin.at[0], zin.at[4])

            rows, cols = yin.shape[1:]
            step = 16 if cols > 2048 else 32

            def squares(i):
                g = yin[own, pl.ds(pl.multiple_of(i * step, step), step), :].astype(F32)
                g = g * g
                part = g[:, :128]
                for j in range(1, cols // 128):
                    part = part + g[:, j * 128 : j * 128 + 128]
                so_far = sq[...]
                for j in range(0, step, 8):
                    so_far = so_far + part[j : j + 8]
                sq[...] = so_far

            each(rows // step, squares)
            pltpu.make_async_copy(yin.at[own], outs[t // 2].at[layer], osem.at[t]).start()

    lz[at.z] = sq[...]
    for k in range(3):
        send(lz.at[at.z], lz.at[at.z], es.at[k], er.at[at.z], line_peers[k])
    for k in (1, 2, 3):
        arrived(lz.at[at.line(k)], er.at[at.line(k)])
    lg[group] = lz[0] + lz[1] + lz[2] + lz[3]
    for k in range(7):
        send(lg.at[group], lg.at[group], es.at[3 + k], er.at[4 + group], group_peers[k])
    for j in others:
        arrived(lg.at[j], er.at[4 + j])
    everything = lg[0]
    for j in range(1, 8):
        everything = everything + lg[j]
    total[...] = everything

    for k in range(3):
        arrived(lz.at[0], es.at[k])
    for k in range(7):
        arrived(lg.at[0], es.at[3 + k])
    for k, name in enumerate(TASKS):
        t, g, p, layer, q, _ = parts(name)
        arrived(p.at[layer, q], cs.at[k])
    for t in range(6):
        bufs, b = (wide, t) if t < 4 else (tall, t - 4)
        for j in range(3):
            arrived(bufs[0].at[b], xs.at[t, j])
            arrived(bufs[0].at[b], ys.at[t, j])
            arrived(bufs[7].at[b, 0], zs.at[t, j])
        arrived(outs[t // 2].at[t % 2], osem.at[t])


def summed(terms):
    DMA = pltpu.SemaphoreType.DMA

    def buffers(n, *block):
        return [pltpu.VMEM((n, k, *block), BF16) for k in (2, 2, 4, 4, 4, 2, 2, 5)] + [pltpu.VMEM((2, 2, 4, *block), BF16)]

    views = [t.reshape(2, 4, 4, 2, t.shape[1] // 32, t.shape[2]) for t in terms]
    blocks = [v.shape[4:] for v in views]
    result = pl.pallas_call(
        rs_kernel,
        out_shape=[jax.ShapeDtypeStruct((2, *b), BF16) for b in blocks]
        + [jax.ShapeDtypeStruct((2, 4, 4, *b), BF16) for b in blocks]
        + [jax.ShapeDtypeStruct((8, 128), F32)],
        in_specs=[ANY] * 3,
        out_specs=[ANY] * 6 + [pl.BlockSpec(memory_space=pltpu.VMEM)],
        scratch_shapes=buffers(4, *blocks[0])
        + buffers(2, *blocks[2])
        + [pltpu.VMEM((8, 128), F32), pltpu.VMEM((4, 8, 128), F32), pltpu.VMEM((8, 8, 128), F32)]
        + [DMA((24,)), DMA((24,)), DMA((2, 2, 2))]
        + [DMA((6, 3))] * 4
        + [DMA((6, 3)), DMA((6, 5)), DMA((6,)), DMA((10,)), DMA((12,))],
        compiler_params=pltpu.CompilerParams(collective_id=0, has_side_effects=True, vmem_limit_bytes=67043328),
        name="sum_terms",
    )(*views)
    return result[:3], jnp.sum(result[6])


def ag_kernel(*refs):
    new, outs = refs[0:3], refs[3:6]
    own, zs, zr, xs, xr, ys, yr, cs, cr = refs[6:]
    at = Place()
    at.meet([at.dev(at.x, at.y, at.line(k), at.c) for k in (1, 2, 3)] + [at.nx, at.ny, at.nc])
    three = range(3)

    def block(t, q, z):
        return outs[t].at[:, q, z, at.c]

    def zj(j):
        if j == 0:
            return at.z
        return at.zi(jnp.where(at.end, j, 0)) if j == 1 else at.zi(j)

    def spread(t, j, src, dst):
        send(src, dst, xs.at[t, j], xr.at[t, j], at.nx)
        send(src, dst, ys.at[t, j], yr.at[t, j], at.ny)
        send(src, dst, cs.at[t, 0, j], cr.at[t, 0, j], at.nc)

    for t in three:
        mine = block(t, at.qo, at.z)

        @pl.when(at.end)
        def _():
            send(new[t], mine, zs.at[t, 0], zr.at[t, 0], at.far)

        @pl.when(at.inner)
        def _():
            send(new[t], mine, zs.at[t, 0], zr.at[t, 1], at.far)
            send(new[t], mine, zs.at[t, 1], zr.at[t, 0], at.near)

        spread(t, 0, new[t], mine)
        pltpu.make_async_copy(new[t], mine, own.at[t]).start()
    for k in three:
        for t in three:
            piece = block(t, at.qo, zj(k + 1))
            arrived(piece, zr.at[t, k])

            @pl.when(at.inner)
            def _():
                if k == 0:
                    send(piece, piece, zs.at[t, 2], zr.at[t, 2], at.far)
                else:
                    send(piece, piece, zs.at[t, 2 + k], zr.at[t, k], at.near)

            spread(t, k + 1, piece, piece)
    for j in range(4):
        for t in three:
            piece = block(t, at.qx, zj(j))
            arrived(piece, xr.at[t, j])
            if j < 2:
                send(piece, piece, ys.at[t, 4 + j], yr.at[t, 4 + j], at.ny)
            send(piece, piece, cs.at[t, 1, j], cr.at[t, 1, j], at.nc)
            piece = block(t, at.qy, zj(j))
            arrived(piece, yr.at[t, j])
            if j >= 2:
                send(piece, piece, xs.at[t, 2 + j], xr.at[t, 2 + j], at.nx)
            send(piece, piece, cs.at[t, 2, j], cr.at[t, 2, j], at.nc)
    for j in range(4):
        for t in three:
            piece = block(t, at.qd, zj(j))
            arrived(piece, yr.at[t, 4 + j] if j < 2 else xr.at[t, 2 + j])
            send(piece, piece, cs.at[t, 3, j], cr.at[t, 3, j], at.nc)
    for t in three:
        piece = block(t, at.qo, at.z)
        for q in range(4):
            for j in range(4):
                arrived(piece, cr.at[t, q, j])
                arrived(piece, cs.at[t, q, j])
        for j in range(6):
            arrived(piece, xs.at[t, j])
            arrived(piece, ys.at[t, j])
        arrived(piece, own.at[t])
        arrived(piece, zs.at[t, 0])

        @pl.when(at.inner)
        def _():
            for j in range(1, 5):
                arrived(piece, zs.at[t, j])


def gathered(new):
    DMA = pltpu.SemaphoreType.DMA
    shapes = [(2, 4, 4, 2, *n.shape[1:]) for n in new]
    result = pl.pallas_call(
        ag_kernel,
        out_shape=[jax.ShapeDtypeStruct(s, BF16) for s in shapes],
        in_specs=[ANY] * 3,
        out_specs=[ANY] * 3,
        scratch_shapes=[DMA((3,)), DMA((3, 5)), DMA((3, 3))] + [DMA((3, 6))] * 4 + [DMA((3, 4, 4))] * 2,
        compiler_params=pltpu.CompilerParams(collective_id=1, has_side_effects=True),
        name="gather_weights",
    )(*new)
    return [r.reshape(2, 32 * n.shape[1], n.shape[2]) for r, n in zip(result, new, strict=True)]


def adamw(w, m, v, g):
    m = 0.9 * m + 0.1 * g
    v = 0.95 * v + 0.05 * g * g
    step = m * lax.rsqrt(v + 1e-8) + 0.1 * w
    return (w - 0.02 * step).astype(BF16), m, v


def solution(mesh):
    def step(*arrays):
        terms, weights, m, v = (arrays[i : i + 3] for i in (0, 3, 6, 9))
        gradients, squares = summed([t[0] for t in terms])
        count = 32 * sum(g.size for g in gradients)
        factor = jnp.minimum(1.0, 0.5 * lax.rsqrt(squares / count + 1e-30))
        me = lax.axis_index("dp")
        own = [lax.dynamic_slice_in_dim(w, me * one.shape[1], one.shape[1], 1).astype(F32) for w, one in zip(weights, m, strict=True)]
        new = [adamw(w, m, v, g.astype(F32) * factor) for w, m, v, g in zip(own, m, v, gradients, strict=True)]
        whole = gathered([one[0] for one in new])
        return (*whole, *(one[1] for one in new), *(one[2] for one in new))

    all_of, cut = P(None, None, None), P(None, "dp", None)
    return jax.shard_map(
        step,
        mesh=mesh,
        in_specs=(P(("rep", "dp"), None, None, None),) * 3 + (all_of,) * 3 + (cut,) * 6,
        out_specs=(P("rep", None, None),) * 3 + (P("rep", "dp", None),) * 6,
        check_vma=False,
    )
```

time: 1200 us -> 621 us (0.52)
  waiting for transfers between devices: 1090 us -> 0 us
  Pallas kernels: 0 us -> 566 us
  blocking collectives: 36.8 us -> 0 us
  between operations: 16.9 us -> 1.47 us
    reduce_scatter x3 -> x0, waiting for transfers between devices: 687 us -> none  [step(): lax.psum_scatter(t[0], 'dp', scatter_dimension=1, tiled=True)]
    pallas_call x0 -> x2, Pallas kernels: none -> 566 us  [the longest x1 300 us: summed(): pl.pallas_call(rs_kernel, out_shape=[jax.ShapeDtypeStruct((2, *b), BF16)...]
    all_gather x3 -> x0, waiting for transfers between devices: 397 us -> none  [step(): whole = [lax.all_gather(one[0], 'dp', axis=1, tiled=True) for one in new]]
    psum x1 -> x0, blocking collectives: 36.8 us -> none  [step(): squares = lax.psum(sum((jnp.sum(g * g) for g in gradients)), 'dp')]
    unnamed x25 -> x27, local copies, waits for them, and re-layouts: 42.3 us -> 42.8 us
  transfers between devices with their start and end apart: 6 -> 0, of which waited for: 6 -> 0; matrix products, arithmetic and copies ran while one was open for 1% -> 0% of each run, Pallas kernels for 0% -> 0%
where the time goes in v1:
time: 621 us
  Pallas kernels  566 us (91%)
  local copies, waits for them, and re-layouts  42.8 us (7%)
  other arithmetic  10.5 us (2%)
    pallas_call x1, Pallas kernels, summed(): pl.pallas_call(rs_kernel, out_shape=[jax.ShapeDtypeStruct((2, *b), BF16)...  300 us
    pallas_call x1, Pallas kernels, gathered(): pl.pallas_call(ag_kernel, out_shape=[jax.ShapeDtypeStruct(s, BF16) for s...  266 us
    unnamed x27, local copies, waits for them, and re-layouts  42.8 us

profile of v1, /device:TPU:0, one launch (start us, length us, event | category | flops | bytes accessed | tf_op | source)
XLA Modules:
  0.0 620.8 jit_solution(9048299528068628749)
XLA Ops:
  0.6 300.2 %sum_terms.1 = (bf16[2,32,5120]{2,1,0:T(8,128)(2,1)}, bf16[2,32,5120]{2,1,0:T(8,128)(2,1)}, bf16[2,160,1024]{2,1,0:T(8,128)(2,1)}, bf16[2,4,4,32,5120]{4,3,2,1,0...) custom-call(bf16[2,4,4,2,32,5120]{5,4,3,2,1,0:T(8,128)(2,1)} %bitcast., ...), custom_call_target="tpu_custom_call" | custom-call | tf_op jit(solution)/shard_map/sum_terms/pallas_call | solution.py:241
  300.8 1.3 reduce_sum.9
  302.8 0.0 copy-start.1
  302.8 0.0 copy-start.2
  302.9 0.0 copy-start.3
  302.9 0.0 copy-start.4
  302.9 0.0 copy-start.5
  302.9 0.0 copy-start.6
  302.9 4.4 fusion.8
  307.3 0.0 copy-done.1
  307.3 0.0 copy-done.2
  307.3 0.0 copy-done.3
  307.3 0.0 copy-done.4
  307.4 0.0 copy-done.5
  307.4 0.6 copy-done.6
  307.9 4.8 fusion.2
  312.7 265.9 %gather_weights.1 = (bf16[2,4,4,2,32,5120]{5,4,3,2,1,0:T(8,128)(2,1)}, bf16[2,4,4,2,32,5120]{5,4,3,2,1,0:T(8,128)(2,1)}, bf16[2,4,4,2,160,1024]{5,4,3,2,1,0:T(8,128)(2,1)}) custom-call(bf16[2,32,5120]{2,1,0:T(8,128)(2,1)} %get-tuple-element.29.refs_0_, bf16[2,32,5120]{2,1,0:T(8,128)(2,1)} %get-tuple-element.32.refs_1_, ...), custom_call_target="tpu_custom_call" | custom-call | tf_op jit(solution)/shard_map/gather_weights/pallas_call | solution.py:345
  578.5 0.0 copy-start
  578.6 0.0 slice-start
  578.6 0.0 slice-start.1
  578.6 0.0 slice-start.2
  578.6 21.0 %copy.24 = bf16[2,1024,5120]{2,1,0:T(8,128)(2,1)} copy(bf16[2,1024,5120]{2,1,0:T(8,128)(2,1)} %bitcast.10) | data formatting | bytes 41943040
  599.5 0.0 copy-done
  599.5 0.0 slice-start.3
  599.5 0.0 slice-start.4
  599.6 10.6 %copy.25 = bf16[2,1024,5120]{2,1,0:T(8,128)(2,1)} copy(bf16[2,1024,5120]{2,1,0:T(8,128)(2,1)S(1)} %bitcast.9) | data formatting | bytes 41943040
  610.2 0.0 slice-done
  610.2 0.0 slice-done.1
  610.2 0.0 slice-done.2
  610.2 1.9 slice-done.3
  612.1 1.2 slice-done.4
  613.3 7.5 %copy.26 = bf16[2,5120,1024]{2,1,0:T(8,128)(2,1)} copy(bf16[2,5120,1024]{2,1,0:T(8,128)(2,1)S(1)} %bitcast.8) | data formatting | bytes 41943040
  (1 shorter events, 0.0 us)
Async XLA Ops:
  302.8 4.5 copy-start.1
  302.8 4.5 copy-start.2
  302.9 4.5 copy-start.3
  302.9 4.5 copy-start.4
  302.9 4.5 copy-start.5
  302.9 5.0 copy-start.6
  578.5 21.0 %copy-start = (bf16[2,4,4,2,32,5120]{5,4,3,2,1,0:T(8,128)(2,1)S(1)}, bf16[2,4,4,2,32,5120]{5,4,3,2,1,0:T(8,128)(2,1)}, u32[]{:S(2)}) copy-start(bf16[2,4,4,2,32,5120]{5,4,3,2,1,0:T(8,128)(2,1)} %get-tuple-element.21) | copy-start | bytes 62914564
  578.6 31.6 %slice-start = ((s8[20971520]{0:T(1024)(128)(4,1)}), s8[4194304]{0:T(1024)(128)(4,1)S(1)}, s32[]{:S(2)}) async-start(s8[20971520]{0:T(1024)(128)(4,1)} %bitcast.6), calls=%async_computation | async-start | bytes 8388608
  578.6 31.6 %slice-start.1 = ((s8[20971520]{0:T(1024)(128)(4,1)}), s8[4194304]{0:T(1024)(128)(4,1)S(1)}, s32[]{:S(2)}) async-start(s8[20971520]{0:T(1024)(128)(4,1)} %bitcast.6), calls=%async_computation.1 | async-start | bytes 8388608
  578.6 31.6 %slice-start.2 = ((s8[20971520]{0:T(1024)(128)(4,1)}), s8[4194304]{0:T(1024)(128)(4,1)S(1)}, s32[]{:S(2)}) async-start(s8[20971520]{0:T(1024)(128)(4,1)} %bitcast.6), calls=%async_computation.2 | async-start | bytes 8388608
  599.5 12.5 %slice-start.3 = ((s8[20971520]{0:T(1024)(128)(4,1)}), s8[4194304]{0:T(1024)(128)(4,1)S(1)}, s32[]{:S(2)}) async-start(s8[20971520]{0:T(1024)(128)(4,1)} %bitcast.6), calls=%async_computation.3 | async-start | bytes 8388608
  599.5 13.7 %slice-start.4 = ((s8[20971520]{0:T(1024)(128)(4,1)}), s8[4194304]{0:T(1024)(128)(4,1)S(1)}, s32[]{:S(2)}) async-start(s8[20971520]{0:T(1024)(128)(4,1)} %bitcast.6), calls=%async_computation.4 | async-start | bytes 8388608

commit v2 on v1

v2 whole, which is shorter than its diff:
```python
import jax
import jax.numpy as jnp
from jax import lax
from jax.experimental import pallas as pl
from jax.experimental.pallas import tpu as pltpu
from jax.sharding import PartitionSpec as P

MESH = pl.DeviceIdType.MESH
F32, BF16 = jnp.float32, jnp.bfloat16
ANY = pl.BlockSpec(memory_space=pl.ANY)


class Place:
    def __init__(self):
        self.rep, d = lax.axis_index("rep"), lax.axis_index("dp")
        self.x, self.y, self.z, self.c = d // 16, lax.rem(d // 8, 2), lax.rem(d // 2, 4), lax.rem(d, 2)
        low = self.z < 2
        self.low = low
        self.mz = jnp.where(low, self.z, 3 - self.z)
        self.end, self.inner = self.mz == 0, self.mz == 1
        self.far = self.dev(self.x, self.y, jnp.where(low, self.z + 1, self.z - 1), self.c)
        self.near = self.dev(self.x, self.y, jnp.where(low, 0, 3), self.c)
        self.nx = self.dev(1 - self.x, self.y, self.z, self.c)
        self.ny = self.dev(self.x, 1 - self.y, self.z, self.c)
        self.nc = self.dev(self.x, self.y, self.z, 1 - self.c)
        self.qo = self.x * 2 + self.y
        self.qx = (1 - self.x) * 2 + self.y
        self.qy = self.x * 2 + 1 - self.y
        self.qd = (1 - self.x) * 2 + 1 - self.y

    def dev(self, x, y, z, c):
        return (self.rep, ((x * 2 + y) * 4 + z) * 2 + c)

    def zi(self, m):
        return jnp.where(self.low, m, 3 - m)

    def line(self, k):
        return lax.rem(self.z + k, 4)

    def meet(self, peers):
        barrier = pltpu.get_barrier_semaphore()
        for p in peers:
            pl.semaphore_signal(barrier, inc=1, device_id=p, device_id_type=MESH)
        pl.semaphore_wait(barrier, len(peers))


def send(src, dst, s, r, to):
    pltpu.make_async_remote_copy(src_ref=src, dst_ref=dst, send_sem=s, recv_sem=r, device_id=to, device_id_type=MESH).start()


def arrived(ref, sem):
    pltpu.make_async_copy(ref, ref, sem).wait()


def add_into(dst, *srcs):
    rows, cols = dst.shape
    step = 16 if cols > 2048 or rows % 32 else 32

    def strip(i, carry):
        at = pl.ds(pl.multiple_of(i * step, step), step)
        total = srcs[0][at, :].astype(F32)
        for s in srcs[1:]:
            total = total + s[at, :].astype(F32)
        dst[at, :] = total.astype(BF16)
        return carry

    lax.fori_loop(0, rows // step, strip, 0)


def each(n, body):
    lax.fori_loop(0, n, lambda i, carry: (body(i), carry)[1], 0)


TASKS = [
    "D4", "D0", "D1", "bS5Y", "D3", "bS5D", "D2", "Y0", "X0", "Y1", "bS5O", "Y2", "X1", "bF5D", "Y3", "bS5X", "X2", "bF5X", "X3", "bF5Y",
    "S0", "F0", "D6", "bH5D", "bH5Y", "S1", "bH5X", "S2", "H0", "F1", "X4", "H1", "F2", "S3", "bF5O", "Y4", "H2", "X6", "Y6", "E2", "bG5D",
    "bG5X", "F3", "bH5O", "E1", "H3", "E0", "S4", "F4", "S6", "bG5Y", "E3", "bK5X", "bK5Y", "H4", "F6", "E4", "H6", "bG5O", "E6",
]
WIDE, LATE = 4, 5


def meaning(name):
    if name[0] == "b":
        return name[:2], int(name[2]), name[3]
    return name[0], int(name[1]), name[0] if name[0] in "DXY" else "O"


def rs_kernel(*refs):
    terms, outs, theirs, total = refs[0:3], refs[3:6], refs[6:9], refs[9]
    wide, tall, late, stages = refs[10:18], refs[18:26], refs[26:34], refs[34:36]
    sq, lz, lg, cs, cr, ls, xs, xr, ys, yr, zs, zr, bzs, bzr, osem, es, er = refs[36:]
    at = Place()
    group = (at.x * 2 + at.y) * 2 + at.c
    line_peers = [at.dev(at.x, at.y, at.line(k), at.c) for k in (1, 2, 3)]
    others = [lax.rem(group + k, 8) for k in range(1, 8)]
    group_peers = [at.dev(j // 4, lax.rem(j // 2, 2), at.z, lax.rem(j, 2)) for j in others]
    at.meet(line_peers + group_peers)
    columns = {"D": at.qd, "X": at.qx, "Y": at.qy, "O": at.qo}
    tall_rows = tall[0].shape[2]

    def source(t):
        if t < WIDE:
            return t // 2, t % 2, pl.ds(0, wide[0].shape[2])
        if t == LATE:
            return 2, 1, pl.ds(0, 2 * tall_rows)
        return 2, 0, pl.ds((t - WIDE) // 2 * tall_rows, tall_rows)

    def half_of(name, c):
        _, t, col = meaning(name)
        weight, layer, rows = source(t)
        return terms[weight].at[layer, columns[col], :, c, rows], theirs[weight].at[layer, columns[col], :, rows]

    first = {}
    for name in TASKS:
        first.setdefault(meaning(name)[1:], name)
    order = list(first.values())
    for k, name in enumerate(order):
        g, p = half_of(name, 1 - at.c)
        send(g, p, cs.at[k], cr.at[k], at.nc)

    slots, used = {}, [0, 0]
    for name in TASKS:
        kind = int(meaning(name)[1] >= WIDE)
        slots[name] = (kind, used[kind] % 2)
        used[kind] += 1

    def staged(name):
        kind, slot = slots[name]
        t = meaning(name)[1]
        rows = pl.ds(0, source(t)[2].size)
        return [(stages[kind].at[slot, k, :, rows], ls.at[kind, slot, k]) for k in range(2)]

    def load(name):
        g, p = half_of(name, at.c)
        (mine, s), (yours, r) = staged(name)
        pltpu.make_async_copy(g, mine, s).start()
        if name in order:
            arrived(p, cr.at[order.index(name)])
        pltpu.make_async_copy(p, yours, r).start()

    def result(t):
        weight, layer, rows = source(t)
        return outs[weight].at[layer, rows]

    def finish(t, done):
        rows, cols = done.shape
        step = 16 if cols > 2048 or rows % 32 else 32

        def squares(i):
            g = done[pl.ds(pl.multiple_of(i * step, step), step), :].astype(F32)
            g = g * g
            part = g[:, :128]
            for j in range(1, cols // 128):
                part = part + g[:, j * 128 : j * 128 + 128]
            so_far = sq[...]
            for j in range(0, step, 8):
                so_far = so_far + part[j : j + 8]
            sq[...] = so_far

        each(rows // step, squares)
        pltpu.make_async_copy(done, result(t), osem.at[t]).start()


    def line_steps(step, zin, s, r, into, start):
        if step == "S":

            @pl.when(at.end)
            def _():
                for m in (3, 2, 1):
                    i = at.zi(m)
                    out = start(m, i)
                    into(out, i)
                    send(out, zin.at[m - 1], s.at[m - 1], r.at[m - 1], at.far)

        elif step == "F":

            @pl.when(at.inner)
            def _():
                for m in (3, 2):
                    arrived(zin.at[m - 1], r.at[m - 1])
                    into(zin.at[m - 1], at.zi(m), zin.at[m - 1])
                    send(zin.at[m - 1], zin.at[6 - m], s.at[m - 1], r.at[6 - m], at.far)

        elif step == "H":

            @pl.when(at.inner)
            def _():
                arrived(zin.at[3], r.at[3])
                into(zin.at[3], at.zi(0), zin.at[3])
                send(zin.at[3], zin.at[3], s.at[0], r.at[3], at.near)

        else:

            @pl.when(at.end)
            def _():
                arrived(zin.at[3], r.at[3])

            @pl.when(at.inner)
            def _():
                arrived(zin.at[0], r.at[0])
                arrived(zin.at[4], r.at[4])

    def plane_first(step, t, mine, yours):
        bufs, b = (wide, t) if t < WIDE else (tall, (t - WIDE) // 2)
        xf, yf, xin, yin, sd, rx, ry, zin = (r.at[b] for r in bufs)
        lower, upper = pl.ds(0, 2), pl.ds(2, 2)
        if step == "D":
            each(4, lambda i: add_into(sd.at[i], mine.at[i], yours.at[i]))
            send(sd.at[lower], xf, xs.at[t, 0], xr.at[t, 0], at.nx)
            send(sd.at[upper], yf, ys.at[t, 0], yr.at[t, 0], at.ny)
        elif step == "X":
            each(2, lambda i: add_into(rx.at[i], mine.at[i], yours.at[i]))
            send(rx, xin.at[lower], xs.at[t, 1], xr.at[t, 1], at.nx)
            arrived(yf, yr.at[t, 0])
            each(2, lambda i: add_into(yf.at[i], mine.at[i + 2], yours.at[i + 2], yf.at[i]))
            send(yf, xin.at[upper], xs.at[t, 2], xr.at[t, 2], at.nx)
        elif step == "Y":
            each(2, lambda i: add_into(ry.at[i], mine.at[i + 2], yours.at[i + 2]))
            send(ry, yin.at[upper], ys.at[t, 1], yr.at[t, 1], at.ny)
            arrived(xf, xr.at[t, 0])
            each(2, lambda i: add_into(xf.at[i], mine.at[i], yours.at[i], xf.at[i]))
            send(xf, yin.at[lower], ys.at[t, 2], yr.at[t, 2], at.ny)
        else:
            if step == "S":
                arrived(xin.at[lower], xr.at[t, 1])
                arrived(yin.at[upper], yr.at[t, 1])
                arrived(yin.at[lower], yr.at[t, 2])
                arrived(xin.at[upper], xr.at[t, 2])

            def into(dst, i, *more):
                add_into(dst, mine.at[i], yours.at[i], xin.at[i], yin.at[i], *more)

            line_steps(step, zin, zs.at[t], zr.at[t], into, lambda m, i: xin.at[i])
            if step == "E":
                own = yin.at[at.z]
                pl.when(at.end)(lambda: into(own, at.z, zin.at[3]))
                pl.when(at.inner)(lambda: into(own, at.z, zin.at[0], zin.at[4]))
                finish(t, own)

    def line_first(step, t, col, mine, yours):
        xf, yf, xin, yin, sd, rx, ry, zins = late
        n = "DXYO".index(col)
        zin = zins.at[n]
        lower, upper = pl.ds(0, tall_rows), pl.ds(tall_rows, tall_rows)

        def summed_z(dst, rows, *more):
            def into(*came):
                add_into(dst, mine.at[at.z, rows], yours.at[at.z, rows], *[zin.at[k, rows] for k in came], *more)

            pl.when(at.end)(lambda: into(3))
            pl.when(at.inner)(lambda: into(0, 4))

        def into(dst, i, *more):
            add_into(dst, mine.at[i], yours.at[i], *more)

        if step != "bK":
            line_steps(step[1], zin, bzs.at[n], bzr.at[n], into, lambda m, i: zin.at[m - 1])
        if step == "bG":
            if col == "D":
                summed_z(sd.at[lower], lower)
                summed_z(sd.at[upper], upper)
                send(sd.at[lower], xf, xs.at[t, 0], xr.at[t, 0], at.nx)
                send(sd.at[upper], yf, ys.at[t, 0], yr.at[t, 0], at.ny)
            elif col == "X":
                summed_z(rx, lower)
                send(rx, xin.at[lower], xs.at[t, 1], xr.at[t, 1], at.nx)
            elif col == "Y":
                summed_z(ry, upper)
                send(ry, yin.at[upper], ys.at[t, 1], yr.at[t, 1], at.ny)
            else:
                arrived(xin.at[lower], xr.at[t, 1])
                arrived(yin.at[upper], yr.at[t, 1])
                arrived(yin.at[lower], yr.at[t, 2])
                arrived(xin.at[upper], xr.at[t, 2])
                summed_z(yin.at[lower], lower, xin.at[lower], yin.at[lower])
                summed_z(yin.at[upper], upper, xin.at[upper], yin.at[upper])
                finish(t, yin)
        elif step == "bK" and col == "X":
            arrived(yf, yr.at[t, 0])
            summed_z(yf, upper, yf)
            send(yf, xin.at[upper], xs.at[t, 2], xr.at[t, 2], at.nx)
        elif step == "bK":
            arrived(xf, xr.at[t, 0])
            summed_z(xf, lower, xf)
            send(xf, yin.at[lower], ys.at[t, 2], yr.at[t, 2], at.ny)

    sq[...] = jnp.zeros_like(sq)
    load(TASKS[0])
    for k, name in enumerate(TASKS):
        if k + 1 < len(TASKS):
            load(TASKS[k + 1])
        step, t, col = meaning(name)
        (mine, s), (yours, r) = staged(name)
        arrived(mine, s)
        arrived(yours, r)
        if t == LATE:
            line_first(step, t, col, mine, yours)
        else:
            plane_first(step, t, mine, yours)

    lz[at.z] = sq[...]
    for k in range(3):
        send(lz.at[at.z], lz.at[at.z], es.at[k], er.at[at.z], line_peers[k])
    for k in (1, 2, 3):
        arrived(lz.at[at.line(k)], er.at[at.line(k)])
    lg[group] = lz[0] + lz[1] + lz[2] + lz[3]
    for k in range(7):
        send(lg.at[group], lg.at[group], es.at[3 + k], er.at[4 + group], group_peers[k])
    for j in others:
        arrived(lg.at[j], er.at[4 + j])
    everything = lg[0]
    for j in range(1, 8):
        everything = everything + lg[j]
    total[...] = everything

    for k in range(3):
        arrived(lz.at[0], es.at[k])
    for k in range(7):
        arrived(lg.at[0], es.at[3 + k])
    for k, name in enumerate(order):
        arrived(half_of(name, at.c)[1], cs.at[k])
    for t in range(7):
        bufs = wide if t < WIDE else tall
        for j in range(3):
            sent = late[0] if t == LATE else bufs[0].at[0]
            arrived(sent, xs.at[t, j])
            arrived(sent, ys.at[t, j])
            if t != LATE:
                arrived(bufs[7].at[0, 0], zs.at[t, j])
            else:
                for n in range(4):
                    arrived(late[7].at[0, 0], bzs.at[n, j])
        arrived(result(t), osem.at[t])


def summed(terms):
    DMA = pltpu.SemaphoreType.DMA

    def buffers(n, *block):
        return [pltpu.VMEM((n, k, *block), BF16) for k in (2, 2, 4, 4, 4, 2, 2, 5)]

    views = [t.reshape(2, 4, 4, 2, t.shape[1] // 32, t.shape[2]) for t in terms]
    blocks = [v.shape[4:] for v in views]
    low, (rows, cols) = blocks[0], blocks[2]
    late = [pltpu.VMEM((n, cols), BF16) for n in (rows // 2, rows // 2, rows, rows, rows, rows // 2, rows // 2)]
    result = pl.pallas_call(
        rs_kernel,
        out_shape=[jax.ShapeDtypeStruct((2, *b), BF16) for b in blocks]
        + [jax.ShapeDtypeStruct((2, 4, 4, *b), BF16) for b in blocks]
        + [jax.ShapeDtypeStruct((8, 128), F32)],
        in_specs=[ANY] * 3,
        out_specs=[ANY] * 6 + [pl.BlockSpec(memory_space=pltpu.VMEM)],
        scratch_shapes=buffers(WIDE, *low)
        + buffers(2, rows // 2, cols)
        + late
        + [pltpu.VMEM((4, 5, rows, cols), BF16)]
        + [pltpu.VMEM((2, 2, 4, *low), BF16), pltpu.VMEM((2, 2, 4, rows, cols), BF16)]
        + [pltpu.VMEM((8, 128), F32), pltpu.VMEM((4, 8, 128), F32), pltpu.VMEM((8, 8, 128), F32)]
        + [DMA((28,)), DMA((28,)), DMA((2, 2, 2))]
        + [DMA((7, 3))] * 4
        + [DMA((7, 3)), DMA((7, 5)), DMA((4, 3)), DMA((4, 5)), DMA((7,)), DMA((10,)), DMA((12,))],
        compiler_params=pltpu.CompilerParams(collective_id=0, has_side_effects=True, vmem_limit_bytes=67043328),
        name="sum_terms",
    )(*views)
    return result[:3], jnp.sum(result[6])


def ag_kernel(*refs):
    new, outs = refs[0:3], refs[3:6]
    own, zs, zr, bzs, bzr, xs, xr, ys, yr, cs, cr = refs[6:]
    at = Place()
    at.meet([at.dev(at.x, at.y, at.line(k), at.c) for k in (1, 2, 3)] + [at.nx, at.ny, at.nc])
    three = range(3)
    columns = (at.qo, at.qx, at.qy, at.qd)
    half = new[2].shape[1] // 2
    lower, upper = pl.ds(0, half), pl.ds(half, half)

    def mine(t):
        return new[t] if t < 2 else new[2].at[t - 2]

    def block(t, q, j):
        if j == 0:
            z = at.z
        else:
            z = at.zi(jnp.where(at.end, j, 0)) if j == 1 else at.zi(j)
        return outs[t].at[:, columns[q], z, at.c] if t < 2 else outs[2].at[t - 2, columns[q], z, at.c]

    def start_line(src, dst, s, r):
        @pl.when(at.end)
        def _():
            send(src, dst, s.at[0], r.at[0], at.far)

        @pl.when(at.inner)
        def _():
            send(src, dst, s.at[0], r.at[1], at.far)
            send(src, dst, s.at[1], r.at[0], at.near)

    def pass_line(k, piece, s, r):
        arrived(piece, r.at[k])

        @pl.when(at.inner)
        def _():
            if k == 0:
                send(piece, piece, s.at[2], r.at[2], at.far)
            else:
                send(piece, piece, s.at[2 + k], r.at[k], at.near)

    def to_core(t, q, j, src, dst):
        send(src, dst, cs.at[t, q, j], cr.at[t, q, j], at.nc)

    def spread(t, j, src, dst):
        send(src, dst, xs.at[t, j], xr.at[t, j], at.nx)
        send(src, dst, ys.at[t, j], yr.at[t, j], at.ny)
        to_core(t, 0, j, src, dst)

    def late_line(k):
        for q in range(4):
            piece = block(3, q, k + 1)
            pass_line(k, piece, bzs.at[q], bzr.at[q])
            to_core(3, q, k + 1, piece, piece)

    def diagonal(j):
        for t in three:
            piece = block(t, 1, j)
            arrived(piece, xr.at[t, j])
            if j < 2:
                send(piece, piece, ys.at[t, 4 + j], yr.at[t, 4 + j], at.ny)
            to_core(t, 1, j, piece, piece)
            piece = block(t, 2, j)
            arrived(piece, yr.at[t, j])
            if j >= 2:
                send(piece, piece, xs.at[t, 2 + j], xr.at[t, 2 + j], at.nx)
            to_core(t, 2, j, piece, piece)

    for t in three:
        start_line(mine(t), block(t, 0, 0), zs.at[t], zr.at[t])
        spread(t, 0, mine(t), block(t, 0, 0))
    spread(3, 0, mine(3), block(3, 0, 0))
    for t in range(4):
        pltpu.make_async_copy(mine(t), block(t, 0, 0), own.at[t]).start()
    for k in three:
        for t in three:
            piece = block(t, 0, k + 1)
            pass_line(k, piece, zs.at[t], zr.at[t])
            spread(t, k + 1, piece, piece)
        if k == 0:
            piece = block(3, 1, 0)
            arrived(piece, xr.at[3, 0])
            send(piece.at[lower], piece.at[lower], ys.at[3, 1], yr.at[3, 1], at.ny)
            to_core(3, 1, 0, piece, piece)
            piece = block(3, 2, 0)
            arrived(piece, yr.at[3, 0])
            send(piece.at[upper], piece.at[upper], xs.at[3, 1], xr.at[3, 1], at.nx)
            to_core(3, 2, 0, piece, piece)
        if k == 1:
            start_line(mine(3), block(3, 0, 0), bzs.at[0], bzr.at[0])
            for q in (1, 2):
                piece = block(3, q, 0)
                start_line(piece, piece, bzs.at[q], bzr.at[q])
    piece = block(3, 3, 0)
    arrived(piece.at[lower], yr.at[3, 1])
    arrived(piece.at[upper], xr.at[3, 1])
    start_line(piece, piece, bzs.at[3], bzr.at[3])
    to_core(3, 3, 0, piece, piece)
    diagonal(0)
    diagonal(1)
    late_line(0)
    diagonal(2)
    late_line(1)
    diagonal(3)
    late_line(2)
    for j in range(4):
        for t in three:
            piece = block(t, 3, j)
            arrived(piece, yr.at[t, 4 + j] if j < 2 else xr.at[t, 2 + j])
            to_core(t, 3, j, piece, piece)

    for t in range(4):
        piece = block(t, 0, 0)
        for q in range(4):
            for j in range(4):
                arrived(piece, cr.at[t, q, j])
                arrived(piece, cs.at[t, q, j])
        arrived(piece, own.at[t])
        for j in range(6 if t < 3 else 1):
            arrived(piece, xs.at[t, j])
            arrived(piece, ys.at[t, j])
        for s in [zs.at[t]] if t < 3 else [bzs.at[q] for q in range(4)]:
            arrived(piece, s.at[0])

            @pl.when(at.inner)
            def _():
                for j in range(1, 5):
                    arrived(piece, s.at[j])

    arrived(block(3, 0, 0).at[lower], xs.at[3, 1])
    arrived(block(3, 0, 0).at[lower], ys.at[3, 1])


def out_kernel(*refs):
    ins, outs, sems = refs[0:3], refs[3:6], refs[6]
    copies = [pltpu.make_async_copy(ins[t].at[layer], outs[t].at[layer], sems.at[t, layer]) for t in range(3) for layer in range(2)]
    for c in copies:
        c.start()
    for c in copies:
        c.wait()


def gathered(new):
    DMA = pltpu.SemaphoreType.DMA
    shapes = [(2, 4, 4, 2, *n.shape[1:]) for n in new]
    VMEM = pl.BlockSpec(memory_space=pltpu.VMEM)
    landed = pl.pallas_call(
        ag_kernel,
        out_shape=[pltpu.VMEM(s, BF16) for s in shapes],
        in_specs=[ANY] * 3,
        out_specs=[VMEM] * 3,
        scratch_shapes=[DMA((4,)), DMA((3, 5)), DMA((3, 3)), DMA((4, 5)), DMA((4, 3))] + [DMA((4, 6))] * 4 + [DMA((4, 4, 4))] * 2,
        compiler_params=pltpu.CompilerParams(collective_id=1, has_side_effects=True, vmem_limit_bytes=1 << 20),
        name="gather_weights",
    )(*new)
    result = pl.pallas_call(
        out_kernel,
        out_shape=[jax.ShapeDtypeStruct(s, BF16) for s in shapes],
        in_specs=[VMEM] * 3,
        out_specs=[ANY] * 3,
        scratch_shapes=[DMA((3, 2))],
        compiler_params=pltpu.CompilerParams(vmem_limit_bytes=1 << 20),
        name="write_weights",
    )(*[pltpu.with_memory_space_constraint(x, pltpu.VMEM) for x in landed])
    return [r.reshape(2, 32 * n.shape[1], n.shape[2]) for r, n in zip(result, new, strict=True)]


def adamw(w, m, v, g):
    m = 0.9 * m + 0.1 * g
    v = 0.95 * v + 0.05 * g * g
    step = m * lax.rsqrt(v + 1e-8) + 0.1 * w
    return (w - 0.02 * step).astype(BF16), m, v


def solution(mesh):
    def step(*arrays):
        terms, weights, m, v = (arrays[i : i + 3] for i in (0, 3, 6, 9))
        gradients, squares = summed([t[0] for t in terms])
        count = 32 * sum(g.size for g in gradients)
        factor = jnp.minimum(1.0, 0.5 * lax.rsqrt(squares / count + 1e-30))
        me = lax.axis_index("dp")
        own = [lax.dynamic_slice_in_dim(w, me * one.shape[1], one.shape[1], 1).astype(F32) for w, one in zip(weights, m, strict=True)]
        new = [adamw(w, m, v, g.astype(F32) * factor) for w, m, v, g in zip(own, m, v, gradients, strict=True)]
        whole = gathered([one[0] for one in new])
        return (*whole, *(one[1] for one in new), *(one[2] for one in new))

    all_of, cut = P(None, None, None), P(None, "dp", None)
    return jax.shard_map(
        step,
        mesh=mesh,
        in_specs=(P(("rep", "dp"), None, None, None),) * 3 + (all_of,) * 3 + (cut,) * 6,
        out_specs=(P("rep", None, None),) * 3 + (P("rep", "dp", None),) * 6,
        check_vma=False,
    )
```

time: 621 us -> 516 us (0.83)
  Pallas kernels: 566 us -> 503 us
  local copies, waits for them, and re-layouts: 42.8 us -> 0.58 us
    pallas_call x1, Pallas kernels: 300 us -> 249 us  [summed(): pl.pallas_call(rs_kernel, out_shape=[jax.ShapeDtypeStruct((2, *b), BF16)...]
    unnamed x27 -> x12, local copies, waits for them, and re-layouts: 42.8 us -> 0.58 us
    pallas_call x1 -> x2, Pallas kernels: 266 us -> 254 us  [the longest x1 234 us: gathered(): pl.pallas_call(ag_kernel, out_shape=[pltpu.VMEM(s, BF16) for s in shapes]...]
where the time goes in v2:
time: 516 us
  Pallas kernels  503 us (97%)
  other arithmetic  10.5 us (2%)
    pallas_call x1, Pallas kernels, summed(): pl.pallas_call(rs_kernel, out_shape=[jax.ShapeDtypeStruct((2, *b), BF16)...  249 us
    pallas_call x1, Pallas kernels, gathered(): pl.pallas_call(ag_kernel, out_shape=[pltpu.VMEM(s, BF16) for s in shapes]...  234 us
    pallas_call x1, Pallas kernels, gathered(): pl.pallas_call(out_kernel, out_shape=[jax.ShapeDtypeStruct(s, BF16) for s...  20.2 us

profile of v2, /device:TPU:0, one launch (start us, length us, event | category | flops | bytes accessed | tf_op | source)
XLA Modules:
  0.0 515.7 jit_solution(2077802034910227764)
XLA Ops:
  0.6 248.9 %sum_terms.1 = (bf16[2,32,5120]{2,1,0:T(8,128)(2,1)}, bf16[2,32,5120]{2,1,0:T(8,128)(2,1)}, bf16[2,160,1024]{2,1,0:T(8,128)(2,1)}, bf16[2,4,4,32,5120]{4,3,2,1,0...) custom-call(bf16[2,4,4,2,32,5120]{5,4,3,2,1,0:T(8,128)(2,1)} %bitcast., ...), custom_call_target="tpu_custom_call" | custom-call | tf_op jit(solution)/shard_map/sum_terms/pallas_call | solution.py:346
  249.5 1.3 reduce_sum.9
  251.5 0.0 copy-start
  251.5 0.0 copy-start.1
  251.5 0.0 copy-start.2
  251.5 0.0 copy-start.3
  251.5 0.0 copy-start.4
  251.6 0.0 copy-start.5
  251.6 4.4 fusion.8
  256.0 0.0 copy-done
  256.0 0.0 copy-done.1
  256.0 0.0 copy-done.2
  256.0 0.0 copy-done.3
  256.0 0.0 copy-done.4
  256.0 0.6 copy-done.5
  256.6 4.8 fusion.2
  261.4 234.0 %gather_weights.1 = (bf16[2,4,4,2,32,5120]{5,4,3,2,1,0:T(8,128)(2,1)S(1)}, bf16[2,4,4,2,32,5120]{5,4,3,2,1,0:T(8,128)(2,1)S(1)}, bf16[2,4,4,2,160,1024]{5,4,3,2,1,0:T(8,128)(2,1)S(1)}) custom-call(bf16[2,32,5120]{2,1,0:T(8,128)(2,1)} %get-tuple-element.35.refs_0_, bf16[2,32,5120]{2,1,0:T(8,128)(2,1)} %get-tuple-element.38.refs_1_, ...), custom_call_target="tpu_custom_call" | custom-call | tf_op jit(solution)/shard_map/gather_weights/pallas_call | solution.py:513
  495.4 20.2 %write_weights.1 = (bf16[2,4,4,2,32,5120]{5,4,3,2,1,0:T(8,128)(2,1)}, bf16[2,4,4,2,32,5120]{5,4,3,2,1,0:T(8,128)(2,1)}, bf16[2,4,4,2,160,1024]{5,4,3,2,1,0:T(8,128)(2,1)}) custom-call(bf16[2,4,4,2,32,5120]{5,4,3,2,1,0:T(8,128)(2,1)S(1)} %get-tuple-element.23.refs_0_, bf16[2,4,4,2,32,5120]{5,4,3,2,1,0:T(8,128)(2,1)S(1)} %get-tuple-element.24.refs_1_, ...), custom_call_target="tpu_custom_call" | custom-call | tf_op jit(solution)/shard_map/write_weights/pallas_call | solution.py:522
Async XLA Ops:
  251.5 4.5 copy-start
  251.5 4.5 copy-start.1
  251.5 4.5 copy-start.2
  251.5 4.5 copy-start.3
  251.5 4.5 copy-start.4
  251.6 5.0 copy-start.5

commit v3 on v2

v3 whole, which is shorter than its diff:
```python
import jax
import jax.numpy as jnp
from jax import lax
from jax.experimental import pallas as pl
from jax.experimental.pallas import tpu as pltpu
from jax.sharding import PartitionSpec as P

MESH = pl.DeviceIdType.MESH
DMA = pltpu.SemaphoreType.DMA
F32, BF16 = jnp.float32, jnp.bfloat16
ANY = pl.BlockSpec(memory_space=pl.ANY)
VMEM = pl.BlockSpec(memory_space=pltpu.VMEM)


class Place:
    def __init__(self):
        self.rep, d = lax.axis_index("rep"), lax.axis_index("dp")
        self.x, self.y, self.z, self.c = d // 16, lax.rem(d // 8, 2), lax.rem(d // 2, 4), lax.rem(d, 2)
        low = self.z < 2
        self.low = low
        self.mz = jnp.where(low, self.z, 3 - self.z)
        self.end, self.inner = self.mz == 0, self.mz == 1
        self.far = self.dev(self.x, self.y, jnp.where(low, self.z + 1, self.z - 1), self.c)
        self.near = self.dev(self.x, self.y, jnp.where(low, 0, 3), self.c)
        self.nx = self.dev(1 - self.x, self.y, self.z, self.c)
        self.ny = self.dev(self.x, 1 - self.y, self.z, self.c)
        self.nc = self.dev(self.x, self.y, self.z, 1 - self.c)
        self.qo = self.x * 2 + self.y
        self.qx = (1 - self.x) * 2 + self.y
        self.qy = self.x * 2 + 1 - self.y
        self.qd = (1 - self.x) * 2 + 1 - self.y

    def dev(self, x, y, z, c):
        return (self.rep, ((x * 2 + y) * 4 + z) * 2 + c)

    def zi(self, m):
        return jnp.where(self.low, m, 3 - m)

    def line(self, k):
        return lax.rem(self.z + k, 4)

    def meet(self, peers):
        barrier = pltpu.get_barrier_semaphore()
        for p in peers:
            pl.semaphore_signal(barrier, inc=1, device_id=p, device_id_type=MESH)
        pl.semaphore_wait(barrier, len(peers))


def send(src, dst, s, r, to):
    pltpu.make_async_remote_copy(src_ref=src, dst_ref=dst, send_sem=s, recv_sem=r, device_id=to, device_id_type=MESH).start()


def arrived(ref, sem):
    pltpu.make_async_copy(ref, ref, sem).wait()


def halves(n):
    return pl.ds(0, n // 2), pl.ds(n // 2, n // 2)


def strips(shape, body):
    rows, cols = shape
    step = 16 if cols > 2048 or rows % 32 else 32

    def strip(i, carry):
        body(pl.ds(pl.multiple_of(i * step, step), step), step)
        return carry

    lax.fori_loop(0, rows // step, strip, 0)


def add_into(dst, *srcs):
    def strip(at, _):
        total = srcs[0][at, :].astype(F32)
        for s in srcs[1:]:
            total = total + s[at, :].astype(F32)
        dst[at, :] = total.astype(BF16)

    strips(dst.shape, strip)


def each(n, body):
    lax.fori_loop(0, n, lambda i, carry: (body(i), carry)[1], 0)


TYPES = [(0, 0, 0, 32), (0, 1, 0, 32), (1, 0, 0, 32), (1, 1, 0, 32), (2, 0, 0, 64), (2, 1, 0, 160), (2, 0, 64, 48), (2, 0, 112, 48)]
LATE = [5, 7]

TASKS = [
    "D4", "D0", "bS7D", "bS5D", "D1", "X0", "bS7O", "bS7Y", "Y0", "bS7X", "D2", "D3", "bF7Y", "bS5X", "Y1", "bF7D", "bS5O", "bF7X", "bH7D",
    "bF7O", "X1", "bF5X", "bF5D", "bH7Y", "Y2", "bS5Y", "X2", "X3", "bF5Y", "Y3", "S0", "D6", "bH5Y", "F0", "bH5D", "S1", "bH7X", "X4",
    "bF5O", "F1", "S2", "bG7D", "H1", "bG7Y", "H0", "F2", "bG5D", "bH5O", "bH5X", "H2", "S3", "E1", "bG7X", "X6", "Y4", "Y6", "F3", "H3",
    "bK7X", "bG5X", "S4", "bK5X", "E2", "bH7O", "bG5Y", "E0", "bK5Y", "F4", "S6", "E3", "bK7Y", "H4", "F6", "E4", "bG7O", "H6", "bG5O",
    "E6",
]


def meaning(name):
    if name[0] == "b":
        return name[:2], int(name[2]), name[3]
    return name[0], int(name[1]), name[0] if name[0] in "DXY" else "O"


def buffers(t, cols):
    rows = TYPES[t][3]
    if t in LATE:
        shapes = [(rows, cols // 2)] * 2 + [(rows, cols)] * 3 + [(rows, cols // 2)] * 2 + [(4, 5, rows, cols)]
    else:
        shapes = [(k, rows, cols) for k in (2, 2, 4, 4, 4, 2, 2, 5)]
    return [pltpu.VMEM(s, BF16) for s in shapes]


def rs_kernel(*refs):
    terms, outs, theirs, total, refs = refs[0:3], refs[3:6], refs[6:9], refs[9], list(refs[10:])
    bufs = [[refs.pop(0) for _ in range(8)] for _ in TYPES]
    stages = refs[:2]
    sq, lz, lg, cs, cr, ls, xs, xr, ys, yr, zs, zr, bzs, bzr, osem, es, er = refs[2:]
    at = Place()
    group = (at.x * 2 + at.y) * 2 + at.c
    line_peers = [at.dev(at.x, at.y, at.line(k), at.c) for k in (1, 2, 3)]
    others = [lax.rem(group + k, 8) for k in range(1, 8)]
    group_peers = [at.dev(j // 4, lax.rem(j // 2, 2), at.z, lax.rem(j, 2)) for j in others]
    at.meet(line_peers + group_peers)
    columns = {"D": at.qd, "X": at.qx, "Y": at.qy, "O": at.qo}

    def half_of(name, c):
        _, t, col = meaning(name)
        weight, layer, row, rows = TYPES[t]
        rows = pl.ds(row, rows)
        return terms[weight].at[layer, columns[col], :, c, rows], theirs[weight].at[layer, columns[col], :, rows]

    first = {}
    for name in TASKS:
        first.setdefault(meaning(name)[1:], name)
    order = list(first.values())
    for k, name in enumerate(order):
        g, p = half_of(name, 1 - at.c)
        send(g, p, cs.at[k], cr.at[k], at.nc)

    slots, used = {}, [0, 0]
    for name in TASKS:
        kind = TYPES[meaning(name)[1]][0] // 2
        slots[name] = (kind, used[kind] % 2)
        used[kind] += 1

    def staged(name):
        kind, slot = slots[name]
        rows = pl.ds(0, TYPES[meaning(name)[1]][3])
        return [(stages[kind].at[slot, k, :, rows], ls.at[kind, slot, k]) for k in range(2)]

    def load(name):
        g, p = half_of(name, at.c)
        (mine, s), (yours, r) = staged(name)
        pltpu.make_async_copy(g, mine, s).start()
        if name in order:
            arrived(p, cr.at[order.index(name)])
        pltpu.make_async_copy(p, yours, r).start()

    def result(t):
        weight, layer, row, rows = TYPES[t]
        return outs[weight].at[layer, pl.ds(row, rows)]

    def finish(t, done):
        def squares(rows, step):
            g = done[rows, :].astype(F32)
            g = g * g
            part = g[:, :128]
            for j in range(128, done.shape[1], 128):
                part = part + g[:, j : j + 128]
            so_far = sq[...]
            for j in range(0, step, 8):
                so_far = so_far + part[j : j + 8]
            sq[...] = so_far

        strips(done.shape, squares)
        pltpu.make_async_copy(done, result(t), osem.at[t]).start()

    def line_steps(step, zin, s, r, into, start):
        def pass_on(k, m, to, k_to, j):
            arrived(zin.at[k], r.at[k])
            into(zin.at[k], at.zi(m), zin.at[k])
            send(zin.at[k], zin.at[k_to], s.at[j], r.at[k_to], to)

        if step == "S":

            @pl.when(at.end)
            def _():
                for m in (3, 2, 1):
                    i = at.zi(m)
                    out = start(m - 1, i)
                    into(out, i)
                    send(out, zin.at[m - 1], s.at[m - 1], r.at[m - 1], at.far)

        elif step == "F":

            @pl.when(at.inner)
            def _():
                for m in (3, 2):
                    pass_on(m - 1, m, at.far, 6 - m, m - 1)

        elif step == "H":
            pl.when(at.inner)(lambda: pass_on(3, 0, at.near, 3, 0))
        else:

            @pl.when(at.end)
            def _():
                arrived(zin.at[3], r.at[3])

            @pl.when(at.inner)
            def _():
                for k in (0, 4):
                    arrived(zin.at[k], r.at[k])

    def run(step, t, col, mine, yours):
        xf, yf, xin, yin, sd, rx, ry, zin = bufs[t]
        late = t in LATE
        lower, upper = halves(xin.shape[0])
        if late:
            n = "DXYO".index(col)
            zin, s, r = zin.at[n], bzs.at[LATE.index(t), n], bzr.at[LATE.index(t), n]
            lower, upper = ((slice(None), cut) for cut in halves(xin.shape[1]))
            everything = (slice(None), slice(None))

            def plane(dst, cut, *more):
                def into(*came):
                    add_into(dst, mine.at[(at.z, *cut)], yours.at[(at.z, *cut)], *[zin.at[(k, *cut)] for k in came], *more)

                pl.when(at.end)(lambda: into(3))
                pl.when(at.inner)(lambda: into(0, 4))

            def into(dst, i, *more):
                add_into(dst, mine.at[i], yours.at[i], *more)
        else:
            s, r = zs.at[t], zr.at[t]
            everything = pl.ds(0, 4)

            def plane(dst, cut, *more):
                each(cut.size, lambda i: add_into(dst.at[i], *[ref.at[i + cut.start] for ref in (mine, yours)], *[ref.at[i] for ref in more]))

            def into(dst, i, *more):
                add_into(dst, mine.at[i], yours.at[i], xin.at[i], yin.at[i], *more)

        to_x = (xin, lower, upper, rx, yf, yr, xs, xr, at.nx)
        to_y = (yin, upper, lower, ry, xf, xr, ys, yr, at.ny)

        def arrivals():
            for dst, raw_cut, cut, _, _, _, _, there, _ in (to_x, to_y):
                arrived(dst.at[raw_cut], there.at[t, 1])
                arrived(dst.at[cut], there.at[t, 2])

        if late and step != "bK":
            line_steps(step[1], zin, s, r, into, lambda k, i: zin.at[k])
        elif not late and step in "SFHE":
            if step == "S":
                arrivals()
            line_steps(step, zin, s, r, into, lambda k, i: xin.at[i])
        if step in ("D", "bG") and col == "D":
            plane(sd, everything)
            send(sd.at[lower], xf, xs.at[t, 0], xr.at[t, 0], at.nx)
            send(sd.at[upper], yf, ys.at[t, 0], yr.at[t, 0], at.ny)
        elif col in "XY" and step in ("X", "Y", "bG", "bK"):
            dst, raw_cut, cut, raw, forward, came, sent, there, to = to_x if col == "X" else to_y
            if step != "bK":
                plane(raw, raw_cut)
                send(raw, dst.at[raw_cut], sent.at[t, 1], there.at[t, 1], to)
            if step != "bG":
                arrived(forward, came.at[t, 0])
                plane(forward, cut, forward)
                send(forward, dst.at[cut], sent.at[t, 2], there.at[t, 2], to)
        elif step == "bG":
            arrivals()
            plane(yin, everything, xin, yin)
            finish(t, yin)
        elif step == "E":
            own = yin.at[at.z]
            pl.when(at.end)(lambda: into(own, at.z, zin.at[3]))
            pl.when(at.inner)(lambda: into(own, at.z, zin.at[0], zin.at[4]))
            finish(t, own)

    sq[...] = jnp.zeros_like(sq)
    load(TASKS[0])
    for k, name in enumerate(TASKS):
        if k + 1 < len(TASKS):
            load(TASKS[k + 1])
        (mine, s), (yours, r) = staged(name)
        arrived(mine, s)
        arrived(yours, r)
        run(*meaning(name), mine, yours)

    lz[at.z] = sq[...]
    for k in range(3):
        send(lz.at[at.z], lz.at[at.z], es.at[k], er.at[at.z], line_peers[k])
    for k in (1, 2, 3):
        arrived(lz.at[at.line(k)], er.at[at.line(k)])
    lg[group] = lz[0] + lz[1] + lz[2] + lz[3]
    for k in range(7):
        send(lg.at[group], lg.at[group], es.at[3 + k], er.at[4 + group], group_peers[k])
    for j in others:
        arrived(lg.at[j], er.at[4 + j])
    everything = lg[0]
    for j in range(1, 8):
        everything = everything + lg[j]
    total[...] = everything

    for k in range(10):
        arrived(lz.at[0], es.at[k])
    for k, name in enumerate(order):
        arrived(half_of(name, at.c)[1], cs.at[k])
    for t in range(len(TYPES)):
        sent, line = bufs[t][0], bufs[t][7]
        for j in range(3):
            arrived(sent, xs.at[t, j])
            arrived(sent, ys.at[t, j])
            if t in LATE:
                for n in range(4):
                    arrived(line.at[0, 0], bzs.at[LATE.index(t), n, j])
            else:
                arrived(line.at[0], zs.at[t, j])
        arrived(result(t), osem.at[t])


def summed(terms):
    views = [t.reshape(2, 4, 4, 2, t.shape[1] // 32, t.shape[2]) for t in terms]
    blocks = [v.shape[4:] for v in views]
    types = len(TYPES)
    result = pl.pallas_call(
        rs_kernel,
        out_shape=[jax.ShapeDtypeStruct((2, *b), BF16) for b in blocks]
        + [jax.ShapeDtypeStruct((2, 4, 4, *b), BF16) for b in blocks]
        + [jax.ShapeDtypeStruct((8, 128), F32)],
        in_specs=[ANY] * 3,
        out_specs=[ANY] * 6 + [VMEM],
        scratch_shapes=[b for t in range(types) for b in buffers(t, blocks[TYPES[t][0]][1])]
        + [pltpu.VMEM((2, 2, 4, *blocks[k]), BF16) for k in (0, 2)]
        + [pltpu.VMEM((*n, 8, 128), F32) for n in ((), (4,), (8,))]
        + [DMA((4 * types,)), DMA((4 * types,)), DMA((2, 2, 2))]
        + [DMA((types, 3))] * 4
        + [DMA((types, 3)), DMA((types, 5)), DMA((2, 4, 3)), DMA((2, 4, 5)), DMA((types,)), DMA((10,)), DMA((12,))],
        compiler_params=pltpu.CompilerParams(collective_id=0, has_side_effects=True, vmem_limit_bytes=67043328),
        name="sum_terms",
    )(*views)
    return result[:3], result[6]


PARTS = [(0, None, 0, 32), (1, None, 0, 32), (2, 0, 0, 112), (2, 1, 0, 160), (2, 0, 112, 48)]

STEPS = [
    "o4", "o3", "o1", "p3", "o0", "o2", "l00", "l10", "s32", "s33", "p4", "l01", "l02", "s42", "s40", "l11", "y10", "l12", "l20", "x02",
    "x20", "s43", "y11", "l22", "b320", "s30", "y20", "s31", "y02", "b301", "l21", "y03", "x11", "b330", "b430", "b300", "b311", "y12",
    "x12", "y13", "b420", "y00", "b302", "s41", "x01", "f20", "b331", "b410", "b432", "x13", "f02", "b421", "y23", "b411", "x00", "b422",
    "x03", "b412", "b321", "y01", "x10", "b401", "b431", "f01", "f11", "b400", "f03", "y21", "x21", "b310", "x22", "y22", "x23", "b332",
    "b402", "b312", "b322", "f10", "f23", "f12", "f00", "f13", "f22", "f21",
]


def ag_kernel(*refs):
    new, outs = refs[0:3], refs[3:6]
    own, zs, zr, bzs, bzr, xs, xr, ys, yr, cs, cr = refs[6:]
    at = Place()
    at.meet([at.dev(at.x, at.y, at.line(k), at.c) for k in (1, 2, 3)] + [at.nx, at.ny, at.nc])
    columns = (at.qo, at.qx, at.qy, at.qd)
    lower, upper = halves(new[2].shape[2])

    def mine(t):
        weight, layer, row, rows = PARTS[t]
        return new[weight] if layer is None else new[weight].at[layer, pl.ds(row, rows)]

    def block(t, q, j):
        weight, layer, row, rows = PARTS[t]
        if j == 0:
            z = at.z
        else:
            z = at.zi(jnp.where(at.end, j, 0)) if j == 1 else at.zi(j)
        if layer is None:
            return outs[weight].at[:, columns[q], z, at.c]
        return outs[weight].at[layer, columns[q], z, at.c, pl.ds(row, rows)]

    def start_line(src, dst, s, r):
        @pl.when(at.end)
        def _():
            send(src, dst, s.at[0], r.at[0], at.far)

        @pl.when(at.inner)
        def _():
            send(src, dst, s.at[0], r.at[1], at.far)
            send(src, dst, s.at[1], r.at[0], at.near)

    def pass_line(k, piece, s, r):
        arrived(piece, r.at[k])

        @pl.when(at.inner)
        def _():
            if k == 0:
                send(piece, piece, s.at[2], r.at[2], at.far)
            else:
                send(piece, piece, s.at[2 + k], r.at[k], at.near)

    def to_core(t, q, j, src, dst):
        send(src, dst, cs.at[t, q, j], cr.at[t, q, j], at.nc)

    def spread(t, j, src, dst):
        send(src, dst, xs.at[t, j], xr.at[t, j], at.nx)
        send(src, dst, ys.at[t, j], yr.at[t, j], at.ny)
        to_core(t, 0, j, src, dst)

    def late(t):
        return bzs.at[t - 3], bzr.at[t - 3]

    def run(kind, t, *rest):
        if kind == "o":
            if t < 3:
                start_line(mine(t), block(t, 0, 0), zs.at[t], zr.at[t])
            spread(t, 0, mine(t), block(t, 0, 0))
        elif kind == "l":
            (k,) = rest
            piece = block(t, 0, k + 1)
            pass_line(k, piece, zs.at[t], zr.at[t])
            spread(t, k + 1, piece, piece)
        elif kind in "xy":
            (j,) = rest
            q, came = (1, xr) if kind == "x" else (2, yr)
            piece = block(t, q, j)
            arrived(piece, came.at[t, j])
            if kind == "x" and j < 2:
                send(piece, piece, ys.at[t, 4 + j], yr.at[t, 4 + j], at.ny)
            if kind == "y" and j >= 2:
                send(piece, piece, xs.at[t, 2 + j], xr.at[t, 2 + j], at.nx)
            to_core(t, q, j, piece, piece)
        elif kind == "f":
            (j,) = rest
            piece = block(t, 3, j)
            arrived(piece, yr.at[t, 4 + j] if j < 2 else xr.at[t, 2 + j])
            to_core(t, 3, j, piece, piece)
        elif kind == "p":
            for q, cut, came, s, r, to in ((1, lower, xr, ys, yr, at.ny), (2, upper, yr, xs, xr, at.nx)):
                piece = block(t, q, 0)
                arrived(piece, came.at[t, 0])
                send(piece.at[:, cut], piece.at[:, cut], s.at[t, 1], r.at[t, 1], to)
                to_core(t, q, 0, piece, piece)
        elif kind == "s":
            (q,) = rest
            piece = block(t, q, 0)
            if q == 3:
                arrived(piece.at[:, lower], yr.at[t, 1])
                arrived(piece.at[:, upper], xr.at[t, 1])
                to_core(t, q, 0, piece, piece)
            s, r = late(t)
            start_line(piece if q else mine(t), piece, s.at[q], r.at[q])
        else:
            q, k = rest
            piece = block(t, q, k + 1)
            s, r = late(t)
            pass_line(k, piece, s.at[q], r.at[q])
            to_core(t, q, k + 1, piece, piece)

    whole = [o.at[:, at.qo, at.z, at.c] for o in outs]
    started = False
    for step in STEPS:
        if step[0] != "o" and not started:
            started = True
            for w in range(3):
                pltpu.make_async_copy(new[w], whole[w], own.at[w]).start()
        run(step[0], *map(int, step[1:]))

    for t in range(len(PARTS)):
        piece = block(t, 0, 0)
        for q in range(4):
            for j in range(4):
                arrived(piece, cr.at[t, q, j])
                arrived(piece, cs.at[t, q, j])
        for j in range(6 if t < 3 else 1):
            arrived(piece, xs.at[t, j])
            arrived(piece, ys.at[t, j])
        if t >= 3:
            arrived(piece.at[:, lower], xs.at[t, 1])
            arrived(piece.at[:, lower], ys.at[t, 1])
        for s in [zs.at[t]] if t < 3 else [late(t)[0].at[q] for q in range(4)]:
            arrived(piece, s.at[0])

            @pl.when(at.inner)
            def _():
                for j in range(1, 5):
                    arrived(piece, s.at[j])

    for w in range(3):
        arrived(whole[w], own.at[w])


def out_kernel(*refs):
    ins, outs, sems = refs[0:3], refs[3:6], refs[6]
    copies = [pltpu.make_async_copy(ins[t].at[layer], outs[t].at[layer], sems.at[t, layer]) for t in range(3) for layer in range(2)]
    for c in copies:
        c.start()
    for c in copies:
        c.wait()


def gathered(new):
    shapes = [(2, 4, 4, 2, *n.shape[1:]) for n in new]
    landed = pl.pallas_call(
        ag_kernel,
        out_shape=[pltpu.VMEM(s, BF16) for s in shapes],
        in_specs=[ANY] * 3,
        out_specs=[VMEM] * 3,
        scratch_shapes=[DMA((3,)), DMA((3, 5)), DMA((3, 3)), DMA((2, 4, 5)), DMA((2, 4, 3))] + [DMA((5, 6))] * 4 + [DMA((5, 4, 4))] * 2,
        compiler_params=pltpu.CompilerParams(collective_id=1, has_side_effects=True, vmem_limit_bytes=1 << 20),
        name="gather_weights",
    )(*new)
    result = pl.pallas_call(
        out_kernel,
        out_shape=[jax.ShapeDtypeStruct(s, BF16) for s in shapes],
        in_specs=[VMEM] * 3,
        out_specs=[ANY] * 3,
        scratch_shapes=[DMA((3, 2))],
        compiler_params=pltpu.CompilerParams(vmem_limit_bytes=1 << 20),
        name="write_weights",
    )(*[pltpu.with_memory_space_constraint(x, pltpu.VMEM) for x in landed])
    return [r.reshape(2, 32 * n.shape[1], n.shape[2]) for r, n in zip(result, new, strict=True)]


def adamw_kernel(count, me, squares, *refs):
    g_in, w_in, m_in, v_in, w_out, m_out, v_out = (refs[i : i + 3] for i in range(0, 21, 3))
    factor = jnp.minimum(1.0, 0.5 * lax.rsqrt(jnp.sum(squares[...], keepdims=True) / count + 1e-30))
    for k in range(3):
        g = g_in[k][0].astype(F32) * factor
        m = 0.9 * m_in[k][0] + 0.1 * g
        v = 0.95 * v_in[k][0] + 0.05 * g * g
        w = w_in[k][0].astype(F32)
        w_out[k][0] = (w - 0.02 * (m * lax.rsqrt(v + 1e-8) + 0.1 * w)).astype(BF16)
        m_out[k][0] = m
        v_out[k][0] = v


def adamw(squares, g, w, m, v):
    cuts = 2
    count = 32 * sum(x.size for x in g)
    sizes = [(1, x.shape[1] // cuts, x.shape[2]) for x in g]
    own = [pl.BlockSpec(s, lambda layer, i, me: (layer, i, 0)) for s in sizes]
    of_all = [pl.BlockSpec(s, lambda layer, i, me: (layer, me[0] * cuts + i, 0)) for s in sizes]
    result = pl.pallas_call(
        lambda *refs: adamw_kernel(count, *refs),
        out_shape=[jax.ShapeDtypeStruct(x.shape, t) for t in (BF16, F32, F32) for x in g],
        grid_spec=pltpu.PrefetchScalarGridSpec(
            num_scalar_prefetch=1,
            grid=(2, cuts),
            in_specs=[pl.BlockSpec(squares.shape, lambda layer, i, me: (0, 0))] + own + of_all + own * 2,
            out_specs=own * 3,
        ),
        name="adamw",
    )(lax.axis_index("dp")[None], squares, *g, *w, *m, *v)
    return result[:3], result[3:6], result[6:]


def solution(mesh):
    def step(*arrays):
        terms, weights, m, v = (arrays[i : i + 3] for i in range(0, 12, 3))
        gradients, squares = summed([t[0] for t in terms])
        new, m, v = adamw(squares, gradients, weights, m, v)
        return (*gathered(new), *m, *v)

    all_of, cut = P(None, None, None), P(None, "dp", None)
    return jax.shard_map(
        step,
        mesh=mesh,
        in_specs=(P(("rep", "dp"), None, None, None),) * 3 + (all_of,) * 3 + (cut,) * 6,
        out_specs=(P("rep", None, None),) * 3 + (P("rep", "dp", None),) * 6,
        check_vma=False,
    )
```

time: 516 us -> 490 us (0.950)
  Pallas kernels: 503 us -> 489 us
  other arithmetic: 10.5 us -> 0 us
    pallas_call x1, Pallas kernels: 234 us -> 222 us  [gathered(): pl.pallas_call(ag_kernel, out_shape=[pltpu.VMEM(s, BF16) for s in shapes]...]
    pallas_call x1, Pallas kernels: 249 us -> 238 us  [summed(): pl.pallas_call(rs_kernel, out_shape=[jax.ShapeDtypeStruct((2, *b), BF16)...]
    convert_element_type x2 -> x0, other arithmetic: 9.2 us -> none  [adamw(): return ((w - 0.02 * step).astype(BF16), m, v)]
    pallas_call x0 -> x1, Pallas kernels: none -> 9.07 us  [adamw(): pl.pallas_call(lambda *refs: adamw_kernel(count, *refs), out_shape=[jax.S...]
where the time goes in v3:
time: 490 us
  Pallas kernels  489 us (100%)
    pallas_call x1, Pallas kernels, summed(): pl.pallas_call(rs_kernel, out_shape=[jax.ShapeDtypeStruct((2, *b), BF16)...  238 us
    pallas_call x1, Pallas kernels, gathered(): pl.pallas_call(ag_kernel, out_shape=[pltpu.VMEM(s, BF16) for s in shapes]...  222 us
    pallas_call x1, Pallas kernels, gathered(): pl.pallas_call(out_kernel, out_shape=[jax.ShapeDtypeStruct(s, BF16) for s...  20.2 us

profile of v3, /device:TPU:0, one launch (start us, length us, event | category | flops | bytes accessed | tf_op | source)
XLA Modules:
  0.0 489.8 jit_solution(15929842387926467312)
XLA Ops:
  0.6 237.9 %sum_terms.1 = (bf16[2,32,5120]{2,1,0:T(8,128)(2,1)}, bf16[2,32,5120]{2,1,0:T(8,128)(2,1)}, bf16[2,160,1024]{2,1,0:T(8,128)(2,1)}, bf16[2,4,4,32,5120]{4,3,2,1,0...) custom-call(bf16[2,4,4,2,32,5120]{5,4,3,2,1,0:T(8,128)(2,1)} %bitcast., ...), custom_call_target="tpu_custom_call" | custom-call | tf_op jit(solution)/shard_map/sum_terms/pallas_call | solution.py:326
  238.6 9.1 %adamw.1 = (bf16[2,32,5120]{2,1,0:T(8,128)(2,1)}, bf16[2,32,5120]{2,1,0:T(8,128)(2,1)}, bf16[2,160,1024]{2,1,0:T(8,128)(2,1)}, f32[2,32,5120]{2,1,0:T(8,128)}, f...) custom-call(s32[1]{0:T(128)} %bitcast.refs_0_, ...), custom_call_target="tpu_custom_call" | custom-call | tf_op jit(solution)/shard_map/adamw/pallas_call | solution.py:540
  247.7 221.8 %gather_weights.1 = (bf16[2,4,4,2,32,5120]{5,4,3,2,1,0:T(8,128)(2,1)S(1)}, bf16[2,4,4,2,32,5120]{5,4,3,2,1,0:T(8,128)(2,1)S(1)}, bf16[2,4,4,2,160,1024]{5,4,3,2,1,0:T(8,128)(2,1)S(1)}) custom-call(bf16[2,32,5120]{2,1,0:T(8,128)(2,1)} %get-tuple-element.32.refs_0_, bf16[2,32,5120]{2,1,0:T(8,128)(2,1)} %get-tuple-element.33.refs_1_, ...), custom_call_target="tpu_custom_call" | custom-call | tf_op jit(solution)/shard_map/gather_weights/pallas_call | solution.py:500
  469.5 20.2 %write_weights.1 = (bf16[2,4,4,2,32,5120]{5,4,3,2,1,0:T(8,128)(2,1)}, bf16[2,4,4,2,32,5120]{5,4,3,2,1,0:T(8,128)(2,1)}, bf16[2,4,4,2,160,1024]{5,4,3,2,1,0:T(8,128)(2,1)}) custom-call(bf16[2,4,4,2,32,5120]{5,4,3,2,1,0:T(8,128)(2,1)S(1)} %get-tuple-element.35.refs_0_, bf16[2,4,4,2,32,5120]{5,4,3,2,1,0:T(8,128)(2,1)S(1)} %get-tuple-element.36.refs_1_, ...), custom_call_target="tpu_custom_call" | custom-call | tf_op jit(solution)/shard_map/write_weights/pallas_call | solution.py:509

commit v4 on v3

--- a/solution.py
+++ b/solution.py
@@ -1,3 +1,5 @@
+import functools
+
 import jax
 import jax.numpy as jnp
 from jax import lax
@@ -83,14 +85,15 @@
     lax.fori_loop(0, n, lambda i, carry: (body(i), carry)[1], 0)
 
 
-TYPES = [(0, 0, 0, 32), (0, 1, 0, 32), (1, 0, 0, 32), (1, 1, 0, 32), (2, 0, 0, 64), (2, 1, 0, 160), (2, 0, 64, 48), (2, 0, 112, 48)]
+TYPES = [(0, 0, 0, 32), (0, 1, 0, 32), (1, 0, 0, 32), (1, 1, 0, 32), (2, 0, 0, 48), (2, 1, 0, 160), (2, 0, 48, 64), (2, 0, 112, 48)]
+SLOTS = 3
 LATE = [5, 7]
 
 TASKS = [
-    "D4", "D0", "bS7D", "bS5D", "D1", "X0", "bS7O", "bS7Y", "Y0", "bS7X", "D2", "D3", "bF7Y", "bS5X", "Y1", "bF7D", "bS5O", "bF7X", "bH7D",
-    "bF7O", "X1", "bF5X", "bF5D", "bH7Y", "Y2", "bS5Y", "X2", "X3", "bF5Y", "Y3", "S0", "D6", "bH5Y", "F0", "bH5D", "S1", "bH7X", "X4",
-    "bF5O", "F1", "S2", "bG7D", "H1", "bG7Y", "H0", "F2", "bG5D", "bH5O", "bH5X", "H2", "S3", "E1", "bG7X", "X6", "Y4", "Y6", "F3", "H3",
-    "bK7X", "bG5X", "S4", "bK5X", "E2", "bH7O", "bG5Y", "E0", "bK5Y", "F4", "S6", "E3", "bK7Y", "H4", "F6", "E4", "bG7O", "H6", "bG5O",
+    "D4", "bS7X", "D2", "bS5Y", "bS5X", "bS7Y", "D0", "D1", "bS7D", "X0", "Y0", "bF5Y", "Y1", "bF5X", "bS5O", "bH5Y", "bS5D", "bH5X", "D3",
+    "Y2", "bF7Y", "X1", "S0", "bS7O", "bH7Y", "X2", "bF7X", "Y3", "bF5O", "bF7D", "bH7D", "X3", "D6", "bH7X", "S1", "F0", "bF5D", "F1",
+    "S2", "bG7D", "bH5O", "H0", "X4", "bH5D", "H1", "F2", "S3", "bG7X", "Y4", "E1", "bF7O", "X6", "H2", "Y6", "bG5D", "F3", "bG5Y", "E0",
+    "bH7O", "bK7X", "S4", "bG7Y", "bG5X", "H3", "E2", "F4", "S6", "bK7Y", "bK5X", "H4", "bK5Y", "F6", "bG7O", "E4", "H6", "E3", "bG5O",
     "E6",
 ]
 
@@ -140,7 +143,7 @@
     slots, used = {}, [0, 0]
     for name in TASKS:
         kind = TYPES[meaning(name)[1]][0] // 2
-        slots[name] = (kind, used[kind] % 2)
+        slots[name] = (kind, used[kind] % SLOTS)
         used[kind] += 1
 
     def staged(name):
@@ -148,13 +151,23 @@
         rows = pl.ds(0, TYPES[meaning(name)[1]][3])
         return [(stages[kind].at[slot, k, :, rows], ls.at[kind, slot, k]) for k in range(2)]
 
+    def where_used(name, body):
+        step = meaning(name)[0][-1]
+        if step in "SFH":
+            pl.when(at.end if step == "S" else at.inner)(body)
+        else:
+            body()
+
     def load(name):
         g, p = half_of(name, at.c)
         (mine, s), (yours, r) = staged(name)
-        pltpu.make_async_copy(g, mine, s).start()
         if name in order:
             arrived(p, cr.at[order.index(name)])
-        pltpu.make_async_copy(p, yours, r).start()
+
+        @functools.partial(where_used, name)
+        def _():
+            pltpu.make_async_copy(g, mine, s).start()
+            pltpu.make_async_copy(p, yours, r).start()
 
     def result(t):
         weight, layer, row, rows = TYPES[t]
@@ -279,12 +292,18 @@
 
     sq[...] = jnp.zeros_like(sq)
     load(TASKS[0])
+    loaded = 1
     for k, name in enumerate(TASKS):
-        if k + 1 < len(TASKS):
-            load(TASKS[k + 1])
+        while loaded < min(len(TASKS), k + (SLOTS if k > len(order) else 2)):
+            load(TASKS[loaded])
+            loaded += 1
         (mine, s), (yours, r) = staged(name)
-        arrived(mine, s)
-        arrived(yours, r)
+
+        @functools.partial(where_used, name)
+        def _():
+            arrived(mine, s)
+            arrived(yours, r)
+
         run(*meaning(name), mine, yours)
 
     lz[at.z] = sq[...]
@@ -331,9 +350,9 @@
         in_specs=[ANY] * 3,
         out_specs=[ANY] * 6 + [VMEM],
         scratch_shapes=[b for t in range(types) for b in buffers(t, blocks[TYPES[t][0]][1])]
-        + [pltpu.VMEM((2, 2, 4, *blocks[k]), BF16) for k in (0, 2)]
+        + [pltpu.VMEM((SLOTS, 2, 4, *blocks[k]), BF16) for k in (0, 2)]
         + [pltpu.VMEM((*n, 8, 128), F32) for n in ((), (4,), (8,))]
-        + [DMA((4 * types,)), DMA((4 * types,)), DMA((2, 2, 2))]
+        + [DMA((4 * types,)), DMA((4 * types,)), DMA((2, SLOTS, 2))]
         + [DMA((types, 3))] * 4
         + [DMA((types, 3)), DMA((types, 5)), DMA((2, 4, 3)), DMA((2, 4, 5)), DMA((types,)), DMA((10,)), DMA((12,))],
         compiler_params=pltpu.CompilerParams(collective_id=0, has_side_effects=True, vmem_limit_bytes=67043328),

time: 490 us -> 488 us (level)
  no operation moved by 1% of the time
where the time goes in v4:
time: 488 us
  Pallas kernels  487 us (100%)
    pallas_call x1, Pallas kernels, summed(): pl.pallas_call(rs_kernel, out_shape=[jax.ShapeDtypeStruct((2, *b), BF16)...  235 us
    pallas_call x1, Pallas kernels, gathered(): pl.pallas_call(ag_kernel, out_shape=[pltpu.VMEM(s, BF16) for s in shapes]...  222 us
    pallas_call x1, Pallas kernels, gathered(): pl.pallas_call(out_kernel, out_shape=[jax.ShapeDtypeStruct(s, BF16) for s...  20.2 us

profile of v4, /device:TPU:0, one launch (start us, length us, event | category | flops | bytes accessed | tf_op | source)
XLA Modules:
  0.0 487.7 jit_solution(11599105192360369786)
XLA Ops:
  0.6 235.4 %sum_terms.1 = (bf16[2,32,5120]{2,1,0:T(8,128)(2,1)}, bf16[2,32,5120]{2,1,0:T(8,128)(2,1)}, bf16[2,160,1024]{2,1,0:T(8,128)(2,1)}, bf16[2,4,4,32,5120]{4,3,2,1,0...) custom-call(bf16[2,4,4,2,32,5120]{5,4,3,2,1,0:T(8,128)(2,1)} %bitcast., ...), custom_call_target="tpu_custom_call" | custom-call | tf_op jit(solution)/shard_map/sum_terms/pallas_call | solution.py:345
  236.1 9.1 %adamw.1 = (bf16[2,32,5120]{2,1,0:T(8,128)(2,1)}, bf16[2,32,5120]{2,1,0:T(8,128)(2,1)}, bf16[2,160,1024]{2,1,0:T(8,128)(2,1)}, f32[2,32,5120]{2,1,0:T(8,128)}, f...) custom-call(s32[1]{0:T(128)} %bitcast.refs_0_, ...), custom_call_target="tpu_custom_call" | custom-call | tf_op jit(solution)/shard_map/adamw/pallas_call | solution.py:559
  245.2 222.1 %gather_weights.1 = (bf16[2,4,4,2,32,5120]{5,4,3,2,1,0:T(8,128)(2,1)S(1)}, bf16[2,4,4,2,32,5120]{5,4,3,2,1,0:T(8,128)(2,1)S(1)}, bf16[2,4,4,2,160,1024]{5,4,3,2,1,0:T(8,128)(2,1)S(1)}) custom-call(bf16[2,32,5120]{2,1,0:T(8,128)(2,1)} %get-tuple-element.32.refs_0_, bf16[2,32,5120]{2,1,0:T(8,128)(2,1)} %get-tuple-element.33.refs_1_, ...), custom_call_target="tpu_custom_call" | custom-call | tf_op jit(solution)/shard_map/gather_weights/pallas_call | solution.py:519
  467.3 20.2 %write_weights.1 = (bf16[2,4,4,2,32,5120]{5,4,3,2,1,0:T(8,128)(2,1)}, bf16[2,4,4,2,32,5120]{5,4,3,2,1,0:T(8,128)(2,1)}, bf16[2,4,4,2,160,1024]{5,4,3,2,1,0:T(8,128)(2,1)}) custom-call(bf16[2,4,4,2,32,5120]{5,4,3,2,1,0:T(8,128)(2,1)S(1)} %get-tuple-element.35.refs_0_, bf16[2,4,4,2,32,5120]{5,4,3,2,1,0:T(8,128)(2,1)S(1)} %get-tuple-element.36.refs_1_, ...), custom_call_target="tpu_custom_call" | custom-call | tf_op jit(solution)/shard_map/write_weights/pallas_call | solution.py:528
